TPU v7x, 32 devices: a 4x4x1 block of a 4x4x8 slice. The times are simulated.
32 devices in a mesh: dp: 1 (over z), tp: 4 (over y), cp: 8 (over x, core).
Axes of the slice: x: 4, y: 4, z: 1, core: 2. Of those that a mesh axis runs over, the one named last changes fastest.
The devices are a block of a 4x4x8 slice.
Arguments:
- hidden: bfloat16 [4096, 4096], P(('dp', 'cp'))
- tok_pos: int32 [4096], P(('dp', 'cp'))
- norm_gain: float32 [4096], replicated
- w_query: bfloat16 [4096, 4096], P(None, 'tp')
- w_key: bfloat16 [4096, 1024], P(None, 'tp')
- w_value: bfloat16 [4096, 1024], P(None, 'tp')
- w_out: bfloat16 [4096, 4096], P('tp')
Outputs:
- output 1: bfloat16 [4096, 4096], P(('dp', 'cp'))
- output 2: bfloat16 [4096, 8, 128], P(('dp', 'cp'), 'tp')
- output 3: bfloat16 [4096, 8, 128], P(('dp', 'cp'), 'tp')
All inputs are finite; a program needn't handle non-finite values.
Results may differ from a plain program's by a relative error of at most 0.00443208.
Values are sent between devices in bfloat16 or wider.
A program may use at most 768 MiB of HBM per device.

v0:
```python
import jax
import jax.numpy as jnp
from jax import lax
from jax.sharding import PartitionSpec as P, NamedSharding

HEAD = 128
THETA = 1000000
EPS = 1e-5
NEG_BIG = -1e30


def rms_normed(hid_f32, norm_gain):
    scaled = hid_f32 * lax.rsqrt(jnp.mean(hid_f32 * hid_f32, axis=-1, keepdims=True) + EPS)
    return (scaled * norm_gain).astype(jnp.bfloat16)


def rope_tables(tok_pos):
    inv_freq = 1.0 / (THETA ** (jnp.arange(0, HEAD, 2, dtype=jnp.float32) / HEAD))
    angles = tok_pos.astype(jnp.float32)[:, None] * inv_freq[None, :]
    return jnp.cos(angles)[:, None, :], jnp.sin(angles)[:, None, :]


def rotate_half(head_vecs, cos_tab, sin_tab):
    half_dim = head_vecs.shape[-1] // 2
    first_half = head_vecs[..., :half_dim].astype(jnp.float32)
    second_half = head_vecs[..., half_dim:].astype(jnp.float32)
    rotated = jnp.concatenate([first_half * cos_tab - second_half * sin_tab, second_half * cos_tab + first_half * sin_tab], axis=-1)
    return rotated.astype(jnp.bfloat16)


def solution(mesh):
    shards = mesh.shape["cp"]
    shift_pairs = [(src, (src + 1) % shards) for src in range(shards)]

    def local_block(hidden, tok_pos, norm_gain, w_query, w_key, w_value, w_out):
        rows, width = hidden.shape
        heads_loc = w_query.shape[1] // HEAD
        kv_loc = w_key.shape[1] // HEAD
        q_per_kv = heads_loc // kv_loc
        attn_scale = HEAD ** -0.5
        hid_f32 = hidden.astype(jnp.float32)
        normed = rms_normed(hid_f32, norm_gain)
        queries = jnp.dot(normed, w_query, preferred_element_type=jnp.float32).astype(jnp.bfloat16).reshape(rows, heads_loc, HEAD)
        keys_raw = jnp.dot(normed, w_key, preferred_element_type=jnp.float32).astype(jnp.bfloat16).reshape(rows, kv_loc, HEAD)
        values = jnp.dot(normed, w_value, preferred_element_type=jnp.float32).astype(jnp.bfloat16).reshape(rows, kv_loc, HEAD)
        cos_tab, sin_tab = rope_tables(tok_pos)
        q_rot = rotate_half(queries, cos_tab, sin_tab).reshape(rows, kv_loc, q_per_kv, HEAD)
        k_rot = rotate_half(keys_raw, cos_tab, sin_tab)

        def absorb(state, k_blk, v_blk, pos_blk):
            row_max, row_sum, acc_ctx = state
            scores = jnp.einsum("qkgd,tkd->kgqt", q_rot, k_blk, preferred_element_type=jnp.float32) * attn_scale
            allowed = pos_blk[None, :] <= tok_pos[:, None]
            scores = jnp.where(allowed, scores, NEG_BIG)
            new_max = jnp.maximum(row_max, jnp.max(scores, axis=-1))
            exp_scores = jnp.exp(scores - new_max[..., None])
            rescale = jnp.exp(row_max - new_max)
            row_sum = row_sum * rescale + jnp.sum(exp_scores, axis=-1)
            acc_ctx = acc_ctx * rescale[..., None] + jnp.einsum("kgqt,tkd->kgqd", exp_scores.astype(jnp.bfloat16), v_blk, preferred_element_type=jnp.float32)
            return new_max, row_sum, acc_ctx

        init_state = (jnp.full((kv_loc, q_per_kv, rows), NEG_BIG, jnp.float32), jnp.zeros((kv_loc, q_per_kv, rows), jnp.float32), jnp.zeros((kv_loc, q_per_kv, rows, HEAD), jnp.float32))
        own_state = absorb(init_state, k_rot, values, tok_pos)

        def step(step_idx, carry):
            k_blk, v_blk, pos_blk, state = carry
            k_blk = lax.ppermute(k_blk, "cp", shift_pairs)
            v_blk = lax.ppermute(v_blk, "cp", shift_pairs)
            pos_blk = lax.ppermute(pos_blk, "cp", shift_pairs)
            return k_blk, v_blk, pos_blk, absorb(state, k_blk, v_blk, pos_blk)

        carry_out = lax.fori_loop(0, shards - 1, step, (k_rot, values, tok_pos, own_state))
        row_max, row_sum, acc_ctx = carry_out[3]
        context = (acc_ctx / row_sum[..., None]).astype(jnp.bfloat16)
        w_out_grid = w_out.reshape(kv_loc, q_per_kv, HEAD, width)
        part_proj = jnp.einsum("kgqd,kgdn->qn", context, w_out_grid, preferred_element_type=jnp.float32)
        attn_proj = lax.psum(part_proj, "tp")
        hidden_out = (hid_f32 + attn_proj).astype(jnp.bfloat16)
        return hidden_out, k_rot, values

    row_spec = P(("dp", "cp"), None)
    cache_spec = P(("dp", "cp"), "tp", None)
    return jax.shard_map(local_block, mesh=mesh, in_specs=(row_spec, P(("dp", "cp")), P(None), P(None, "tp"), P(None, "tp"), P(None, "tp"), P("tp", None)), out_specs=(row_spec, cache_spec, cache_spec), check_vma=False)
```

profile of v0, /device:TPU:97, one launch (start us, length us, event | category | flops | bytes accessed | tf_op | source)
XLA Modules:
  0.0 332.8 jit_solution(11946471027225498009)
XLA Ops:
  9.8 3.1 fusion.13
  12.9 3.8 %convolution_convert_fusion.1 = bf16[512,256]{0,1:T(8,128)(2,1)S(1)} fusion(bf16[4096,256]{1,0:T(8,128)(2,1)S(1)} %copy-done, bf16[512,4096]{1,0:T(8,128)(2,1)} %param.9, f32[4096]{0:T(1024)} %param.11, f32[512]{0:T(512)S(1)} %add_rsqrt_fusion), kind=kOutput, calls=%fused_computation.40 | convolution fusion | flops 1082261504 | bytes 6572032 | tf_op jit(solution)/shard_map/dot_general | solution.py:45
  18.3 4.4 %convolution_convert_fusion.2 = bf16[512,256]{0,1:T(8,128)(2,1)S(1)} fusion(bf16[4096,256]{1,0:T(8,128)(2,1)} %param.13, bf16[512,4096]{1,0:T(8,128)(2,1)} %param.9, f32[4096]{0:T(1024)S(1)} %copy-done.9, f32[512]{0:T(512)S(1)} %add_rsqrt_fusion), kind=kOutput, calls=%fused_computation.41 | convolution fusion | flops 1082261504 | bytes 6572032 | tf_op jit(solution)/shard_map/dot_general | solution.py:44
  23.5 9.3 %convolution_convert_fusion = bf16[512,1024]{1,0:T(8,128)(2,1)S(1)} fusion(bf16[4096,1024]{1,0:T(8,128)(2,1)} %param.12, bf16[512,4096]{1,0:T(8,128)(2,1)} %param.9, f32[4096]{0:T(1024)S(1)} %copy-done.9, f32[512]{0:T(512)S(1)} %add_rsqrt_fusion), kind=kOutput, calls=%fused_computation.35 | convolution fusion | flops 4303880192 | bytes 13649920 | tf_op jit(solution)/shard_map/dot_general | solution.py:43
  37.2 2.5 fusion.24
  41.6 3.9 %fusion.28 = f32[2,4,512,128]{3,2,1,0:T(8,128)} fusion(bf16[512,2,128,1]{0,2,3,1:T(8,128)(2,1)S(1)} %bitcast.98, f32[2,512,512,4]{2,1,3,0:T(8,128)S(1)} %get-tuple-element.110, f32[2,4,512]{2,1,0:T(4,128)S(1)} %broadcast_maximum_fusion, pred[512,512]{0,1:T(8,128)(4,1)S(1)} %broadcast_compare_fusion.1, f32[2,4,512]{2,1,0:T(4,128)S(1)} %get-tuple-element.105), kind=kOutput, calls=%fused_computation.34 | convolution fusion | flops 545783808 | bytes 11042816 | tf_op jit(solution)/shard_map/kgqt,tkd->kgqd/dot_general | solution.py:59
  45.5 102.7 %while.20 = (s32[]{:T(128)}, bf16[512,2,128]{2,0,1:T(8,128)(2,1)S(1)}, bf16[512,2,128]{2,0,1:T(8,128)(2,1)S(1)}, s32[512]{0:T(512)S(1)}, f32[2,4,512]{2,1,0:T(4,...) while((s32[]{:T(128)}, ...), condition=%wide.region_6.7_spmd, body=%wide.region_3.6_spmd.sunk | while | flops 1098129408 | bytes 52183316 | solution.py:72
  45.5 2.7 collective-permute-start
  55.2 3.2 multiply_add_fusion.5
  59.8 2.5 collective-permute-start
  69.2 3.2 multiply_add_fusion.5
  73.8 2.5 collective-permute-start
  83.3 3.2 multiply_add_fusion.5
  87.8 2.5 collective-permute-start
  98.0 3.2 multiply_add_fusion.5
  106.1 3.5 %collective-permute-done.2 = s32[512]{0:T(512)S(1)} collective-permute-done((s32[512]{0:T(512)S(1)}, s32[512]{0:T(512)S(1)}, u32[]{:S(2)}, u32[]{:S(2)}) %collective-permute-start.2) | collective-permute-done | bytes 2080 | tf_op jit(solution)/shard_map/while/body/eval_jaxpr/ppermute | solution.py:69
  113.2 3.2 multiply_add_fusion.5
  120.1 4.7 %collective-permute-done.2 = s32[512]{0:T(512)S(1)} collective-permute-done((s32[512]{0:T(512)S(1)}, s32[512]{0:T(512)S(1)}, u32[]{:S(2)}, u32[]{:S(2)}) %collective-permute-start.2) | collective-permute-done | bytes 2080 | tf_op jit(solution)/shard_map/while/body/eval_jaxpr/ppermute | solution.py:69
  128.4 3.2 multiply_add_fusion.5
  134.1 5.9 %collective-permute-done.2 = s32[512]{0:T(512)S(1)} collective-permute-done((s32[512]{0:T(512)S(1)}, s32[512]{0:T(512)S(1)}, u32[]{:S(2)}, u32[]{:S(2)}) %collective-permute-start.2) | collective-permute-done | bytes 2080 | tf_op jit(solution)/shard_map/while/body/eval_jaxpr/ppermute | solution.py:69
  143.7 3.2 multiply_add_fusion.5
  148.2 9.7 %fusion.21 = f32[512,4096]{1,0:T(8,128)} fusion(bf16[2,4,128,4096]{3,2,1,0:T(8,128)(2,1)} %bitcast.104, f32[2,4,512,128]{3,2,1,0:T(8,128)} %get-tuple-element.51, f32[2,4,512]{2,1,0:T(4,128)S(1)} %get-tuple-element.52), kind=kOutput, calls=%fused_computation.29 | convolution fusion | flops 4296015872 | bytes 18890752 | tf_op jit(solution)/shard_map/kgqd,kgdn->qn/dot_general | solution.py:76
  159.8 158.1 %all-reduce.2.cloned.1.call-done = f32[512,4096]{1,0:T(8,128)} async-done(((f32[512,4096]{1,0:T(8,128)}), f32[512,4096]{1,0:T(8,128)}) %all-reduce.2.cloned.1.call-update) | async-done | bytes 8388624 | tf_op jit(solution)/shard_map/psum | solution.py:77
  317.9 8.0 %fusion.16 = bf16[512,4096]{1,0:T(8,128)(2,1)} fusion(f32[512,4096]{1,0:T(8,128)} %all-reduce.2.cloned.1.call-done, bf16[512,4096]{1,0:T(8,128)(2,1)} %param.9), kind=kLoop, calls=%fused_computation.22 | loop fusion | flops 6291456 | bytes 16777216 | tf_op jit(solution)/shard_map/convert_element_type | solution.py:78
  (172 shorter events, 68.3 us)
Async XLA Ops:
  7.2 310.7 %all-reduce.2.cloned.1.call-start = ((), (), s32[]{:S(2)}) async-start(), calls=%async_computation | async-start | bytes 16777216 | tf_op jit(solution)/shard_map/psum | solution.py:77
  23.5 9.3 %copy-start.2 = (bf16[512,2,128]{2,0,1:T(8,128)(2,1)}, bf16[512,2,128]{2,0,1:T(8,128)(2,1)S(1)}, u32[]{:S(2)}) copy-start(bf16[512,2,128]{2,0,1:T(8,128)(2,1)S(1)} %pad_maximum_fusion.1) | copy-start | bytes 786436
  45.5 6.3 %collective-permute-start = (bf16[512,2,128]{2,0,1:T(8,128)(2,1)S(1)}, bf16[512,2,128]{2,0,1:T(8,128)(2,1)S(1)}, u32[]{:S(2)}, u32[]{:S(2)}) collective-permute-start(bf16[512,2,128]{2,0,1:T(8,128)(2,1)S(1)} %get-tuple-element.189), channel_id=1, source_target_pairs={{0,1},{1,2},{2,3},{3,4},{4,5},{5,6},{6,7},{7,0},{8,9},{9,10},{10,1... | collective-permute-start | bytes 786440 | tf_op jit(solution)/shard_map/while/body/eval_jaxpr/ppermute | solution.py:67
  48.3 3.3 collective-permute-start.2
  48.3 6.9 %collective-permute-start.1 = (bf16[512,2,128]{2,0,1:T(8,128)(2,1)S(1)}, bf16[512,2,128]{2,0,1:T(8,128)(2,1)S(1)}, u32[]{:S(2)}, u32[]{:S(2)}) collective-permute-start(bf16[512,2,128]{2,0,1:T(8,128)(2,1)S(1)} %get-tuple-element.190), channel_id=1, source_target_pairs={{0,1},{1,2},{2,3},{3,4},{4,5},{5,6},{6,7},{7,0},{8,9},{9,10},{10,1... | collective-permute-start | bytes 786440 | tf_op jit(solution)/shard_map/while/body/eval_jaxpr/ppermute | solution.py:68
  59.8 6.0 %collective-permute-start = (bf16[512,2,128]{2,0,1:T(8,128)(2,1)S(1)}, bf16[512,2,128]{2,0,1:T(8,128)(2,1)S(1)}, u32[]{:S(2)}, u32[]{:S(2)}) collective-permute-start(bf16[512,2,128]{2,0,1:T(8,128)(2,1)S(1)} %get-tuple-element.189), channel_id=1, source_target_pairs={{0,1},{1,2},{2,3},{3,4},{4,5},{5,6},{6,7},{7,0},{8,9},{9,10},{10,1... | collective-permute-start | bytes 786440 | tf_op jit(solution)/shard_map/while/body/eval_jaxpr/ppermute | solution.py:67
  62.3 3.3 collective-permute-start.2
  62.3 6.9 %collective-permute-start.1 = (bf16[512,2,128]{2,0,1:T(8,128)(2,1)S(1)}, bf16[512,2,128]{2,0,1:T(8,128)(2,1)S(1)}, u32[]{:S(2)}, u32[]{:S(2)}) collective-permute-start(bf16[512,2,128]{2,0,1:T(8,128)(2,1)S(1)} %get-tuple-element.190), channel_id=1, source_target_pairs={{0,1},{1,2},{2,3},{3,4},{4,5},{5,6},{6,7},{7,0},{8,9},{9,10},{10,1... | collective-permute-start | bytes 786440 | tf_op jit(solution)/shard_map/while/body/eval_jaxpr/ppermute | solution.py:68
  73.8 6.0 %collective-permute-start = (bf16[512,2,128]{2,0,1:T(8,128)(2,1)S(1)}, bf16[512,2,128]{2,0,1:T(8,128)(2,1)S(1)}, u32[]{:S(2)}, u32[]{:S(2)}) collective-permute-start(bf16[512,2,128]{2,0,1:T(8,128)(2,1)S(1)} %get-tuple-element.189), channel_id=1, source_target_pairs={{0,1},{1,2},{2,3},{3,4},{4,5},{5,6},{6,7},{7,0},{8,9},{9,10},{10,1... | collective-permute-start | bytes 786440 | tf_op jit(solution)/shard_map/while/body/eval_jaxpr/ppermute | solution.py:67
  76.3 3.3 collective-permute-start.2
  76.3 6.9 %collective-permute-start.1 = (bf16[512,2,128]{2,0,1:T(8,128)(2,1)S(1)}, bf16[512,2,128]{2,0,1:T(8,128)(2,1)S(1)}, u32[]{:S(2)}, u32[]{:S(2)}) collective-permute-start(bf16[512,2,128]{2,0,1:T(8,128)(2,1)S(1)} %get-tuple-element.190), channel_id=1, source_target_pairs={{0,1},{1,2},{2,3},{3,4},{4,5},{5,6},{6,7},{7,0},{8,9},{9,10},{10,1... | collective-permute-start | bytes 786440 | tf_op jit(solution)/shard_map/while/body/eval_jaxpr/ppermute | solution.py:68
  87.8 6.8 %collective-permute-start = (bf16[512,2,128]{2,0,1:T(8,128)(2,1)S(1)}, bf16[512,2,128]{2,0,1:T(8,128)(2,1)S(1)}, u32[]{:S(2)}, u32[]{:S(2)}) collective-permute-start(bf16[512,2,128]{2,0,1:T(8,128)(2,1)S(1)} %get-tuple-element.189), channel_id=1, source_target_pairs={{0,1},{1,2},{2,3},{3,4},{4,5},{5,6},{6,7},{7,0},{8,9},{9,10},{10,1... | collective-permute-start | bytes 786440 | tf_op jit(solution)/shard_map/while/body/eval_jaxpr/ppermute | solution.py:67
  90.3 4.0 %collective-permute-start.2 = (s32[512]{0:T(512)S(1)}, s32[512]{0:T(512)S(1)}, u32[]{:S(2)}, u32[]{:S(2)}) collective-permute-start(s32[512]{0:T(512)S(1)} %get-tuple-element.191), channel_id=1, source_target_pairs={{0,1},{1,2},{2,3},{3,4},{4,5},{5,6},{6,7},{7,0},{8,9},{9,10},{10,1... | collective-permute-start | bytes 6152 | tf_op jit(solution)/shard_map/while/body/eval_jaxpr/ppermute | solution.py:69
  90.3 7.6 %collective-permute-start.1 = (bf16[512,2,128]{2,0,1:T(8,128)(2,1)S(1)}, bf16[512,2,128]{2,0,1:T(8,128)(2,1)S(1)}, u32[]{:S(2)}, u32[]{:S(2)}) collective-permute-start(bf16[512,2,128]{2,0,1:T(8,128)(2,1)S(1)} %get-tuple-element.190), channel_id=1, source_target_pairs={{0,1},{1,2},{2,3},{3,4},{4,5},{5,6},{6,7},{7,0},{8,9},{9,10},{10,1... | collective-permute-start | bytes 786440 | tf_op jit(solution)/shard_map/while/body/eval_jaxpr/ppermute | solution.py:68
  102.5 7.3 %collective-permute-start = (bf16[512,2,128]{2,0,1:T(8,128)(2,1)S(1)}, bf16[512,2,128]{2,0,1:T(8,128)(2,1)S(1)}, u32[]{:S(2)}, u32[]{:S(2)}) collective-permute-start(bf16[512,2,128]{2,0,1:T(8,128)(2,1)S(1)} %get-tuple-element.189), channel_id=1, source_target_pairs={{0,1},{1,2},{2,3},{3,4},{4,5},{5,6},{6,7},{7,0},{8,9},{9,10},{10,1... | collective-permute-start | bytes 786440 | tf_op jit(solution)/shard_map/while/body/eval_jaxpr/ppermute | solution.py:67
  104.3 5.2 %collective-permute-start.2 = (s32[512]{0:T(512)S(1)}, s32[512]{0:T(512)S(1)}, u32[]{:S(2)}, u32[]{:S(2)}) collective-permute-start(s32[512]{0:T(512)S(1)} %get-tuple-element.191), channel_id=1, source_target_pairs={{0,1},{1,2},{2,3},{3,4},{4,5},{5,6},{6,7},{7,0},{8,9},{9,10},{10,1... | collective-permute-start | bytes 6152 | tf_op jit(solution)/shard_map/while/body/eval_jaxpr/ppermute | solution.py:69
  104.3 8.8 %collective-permute-start.1 = (bf16[512,2,128]{2,0,1:T(8,128)(2,1)S(1)}, bf16[512,2,128]{2,0,1:T(8,128)(2,1)S(1)}, u32[]{:S(2)}, u32[]{:S(2)}) collective-permute-start(bf16[512,2,128]{2,0,1:T(8,128)(2,1)S(1)} %get-tuple-element.190), channel_id=1, source_target_pairs={{0,1},{1,2},{2,3},{3,4},{4,5},{5,6},{6,7},{7,0},{8,9},{9,10},{10,1... | collective-permute-start | bytes 786440 | tf_op jit(solution)/shard_map/while/body/eval_jaxpr/ppermute | solution.py:68
  117.7 7.3 %collective-permute-start = (bf16[512,2,128]{2,0,1:T(8,128)(2,1)S(1)}, bf16[512,2,128]{2,0,1:T(8,128)(2,1)S(1)}, u32[]{:S(2)}, u32[]{:S(2)}) collective-permute-start(bf16[512,2,128]{2,0,1:T(8,128)(2,1)S(1)} %get-tuple-element.189), channel_id=1, source_target_pairs={{0,1},{1,2},{2,3},{3,4},{4,5},{5,6},{6,7},{7,0},{8,9},{9,10},{10,1... | collective-permute-start | bytes 786440 | tf_op jit(solution)/shard_map/while/body/eval_jaxpr/ppermute | solution.py:67
  118.3 6.5 %collective-permute-start.2 = (s32[512]{0:T(512)S(1)}, s32[512]{0:T(512)S(1)}, u32[]{:S(2)}, u32[]{:S(2)}) collective-permute-start(s32[512]{0:T(512)S(1)} %get-tuple-element.191), channel_id=1, source_target_pairs={{0,1},{1,2},{2,3},{3,4},{4,5},{5,6},{6,7},{7,0},{8,9},{9,10},{10,1... | collective-permute-start | bytes 6152 | tf_op jit(solution)/shard_map/while/body/eval_jaxpr/ppermute | solution.py:69
  118.3 10.1 %collective-permute-start.1 = (bf16[512,2,128]{2,0,1:T(8,128)(2,1)S(1)}, bf16[512,2,128]{2,0,1:T(8,128)(2,1)S(1)}, u32[]{:S(2)}, u32[]{:S(2)}) collective-permute-start(bf16[512,2,128]{2,0,1:T(8,128)(2,1)S(1)} %get-tuple-element.190), channel_id=1, source_target_pairs={{0,1},{1,2},{2,3},{3,4},{4,5},{5,6},{6,7},{7,0},{8,9},{9,10},{10,1... | collective-permute-start | bytes 786440 | tf_op jit(solution)/shard_map/while/body/eval_jaxpr/ppermute | solution.py:68
  133.0 7.3 %collective-permute-start = (bf16[512,2,128]{2,0,1:T(8,128)(2,1)S(1)}, bf16[512,2,128]{2,0,1:T(8,128)(2,1)S(1)}, u32[]{:S(2)}, u32[]{:S(2)}) collective-permute-start(bf16[512,2,128]{2,0,1:T(8,128)(2,1)S(1)} %get-tuple-element.189), channel_id=1, source_target_pairs={{0,1},{1,2},{2,3},{3,4},{4,5},{5,6},{6,7},{7,0},{8,9},{9,10},{10,1... | collective-permute-start | bytes 786440 | tf_op jit(solution)/shard_map/while/body/eval_jaxpr/ppermute | solution.py:67
  133.0 7.0 %collective-permute-start.2 = (s32[512]{0:T(512)S(1)}, s32[512]{0:T(512)S(1)}, u32[]{:S(2)}, u32[]{:S(2)}) collective-permute-start(s32[512]{0:T(512)S(1)} %get-tuple-element.191), channel_id=1, source_target_pairs={{0,1},{1,2},{2,3},{3,4},{4,5},{5,6},{6,7},{7,0},{8,9},{9,10},{10,1... | collective-permute-start | bytes 6152 | tf_op jit(solution)/shard_map/while/body/eval_jaxpr/ppermute | solution.py:69
  133.0 10.6 %collective-permute-start.1 = (bf16[512,2,128]{2,0,1:T(8,128)(2,1)S(1)}, bf16[512,2,128]{2,0,1:T(8,128)(2,1)S(1)}, u32[]{:S(2)}, u32[]{:S(2)}) collective-permute-start(bf16[512,2,128]{2,0,1:T(8,128)(2,1)S(1)} %get-tuple-element.190), channel_id=1, source_target_pairs={{0,1},{1,2},{2,3},{3,4},{4,5},{5,6},{6,7},{7,0},{8,9},{9,10},{10,1... | collective-permute-start | bytes 786440 | tf_op jit(solution)/shard_map/while/body/eval_jaxpr/ppermute | solution.py:68
  158.8 167.1 %copy-start.1 = (bf16[4096,256]{1,0:T(8,128)(2,1)S(1)}, bf16[4096,256]{1,0:T(8,128)(2,1)}, u32[]{:S(2)}) copy-start(bf16[4096,256]{1,0:T(8,128)(2,1)} %param.14) | copy-start | bytes 6291460
  (22 other events, 67.6 us)
Sparse Core Ops, SparseCore 0:
  158.1 159.8 all-reduce.1
where the time goes:
time: 333 us
  waiting for transfers between devices  179 us (54%)
  matrix products  66.6 us (20%)
  other arithmetic  31.2 us (9%)
  starting transfers between devices  24.4 us (7%)
  local copies, waits for them, and re-layouts  16.4 us (5%)
  between operations  14.3 us (4%)
    psum x1, waiting for transfers between devices, local_block(): attn_proj = lax.psum(part_proj, 'tp')  158 us
    dot_general x8, matrix products, absorb(): jnp.einsum('kgqt,tkd->kgqd', exp_scores.astype(jnp.bfloat16), v_blk, pref...  26.3 us
    ppermute x7, waiting for transfers between devices, step(): pos_blk = lax.ppermute(pos_blk, 'cp', shift_pairs)  21 us
    reduce_sum x8, other arithmetic, absorb(): row_sum = row_sum * rescale + jnp.sum(exp_scores, axis=-1)  14.2 us
    dot_general x8, matrix products, absorb(): jnp.einsum('qkgd,tkd->kgqt', q_rot, k_blk, preferred_element_type=jnp.flo...  13.1 us
    ppermute x7, starting transfers between devices, step(): k_blk = lax.ppermute(k_blk, 'cp', shift_pairs)  12.6 us
    ppermute x7, starting transfers between devices, step(): v_blk = lax.ppermute(v_blk, 'cp', shift_pairs)  11.6 us
    dot_general x1, matrix products, local_block(): jnp.einsum('kgqd,kgdn->qn', context, w_out_grid, preferred_element_type=j...  9.68 us
  transfers between devices with their start and end apart: 22, of which 8 were waited for; matrix products, arithmetic and copies ran while one was open for 8% of the time, Pallas kernels for 0%

commit v1 on v0

v1 whole, which is shorter than its diff:
```python
import functools

import jax
import jax.numpy as jnp
from jax import lax
from jax.experimental import pallas as pl
from jax.experimental.pallas import tpu as pltpu
from jax.sharding import PartitionSpec as P

HEAD = 128
THETA = 1000000
EPS = 1e-5
NEG_BIG = -1e30
LOG2E = 1.4426950408889634
MESH = pl.DeviceIdType.MESH
VMEM_LIMIT = 64 * 2**20 - 64 * 2**10
POS_ROWS = 16
POS_BASE = 64


def vmem_spec():
    return pl.BlockSpec(memory_space=pltpu.VMEM)


def any_spec():
    return pl.BlockSpec(memory_space=pl.ANY)


def rope_tables(tok_pos):
    inv_freq = 1.0 / (THETA ** (jnp.arange(0, HEAD, 2, dtype=jnp.float32) / HEAD))
    angles = tok_pos.astype(jnp.float32)[:, None] * inv_freq[None, :]
    cos, sin = jnp.cos(angles), jnp.sin(angles)
    return jnp.concatenate([cos, cos], axis=-1), jnp.concatenate([-sin, sin], axis=-1)


def rope(head_f32, cos_full, sin_full):
    vals = head_f32.astype(jnp.bfloat16).astype(jnp.float32)
    return (vals * cos_full + pltpu.roll(vals, HEAD // 2, 1) * sin_full).astype(jnp.bfloat16)


def norm_kv_kernel(hid_ref, gain_ref, wk_ref, wv_ref, cos_ref, sin_ref, r_ref, k_ref, v_ref):
    x = hid_ref[...].astype(jnp.float32)
    scaled = x * lax.rsqrt(jnp.mean(x * x, axis=-1, keepdims=True) + EPS)
    normed = (scaled * gain_ref[...]).astype(jnp.bfloat16)
    r_ref[...] = normed
    k = jnp.dot(normed, wk_ref[...], preferred_element_type=jnp.float32)
    for h in range(k.shape[1] // HEAD):
        cols = slice(h * HEAD, (h + 1) * HEAD)
        k_ref[:, cols] = rope(k[:, cols], cos_ref[...], sin_ref[...])
    v_ref[...] = jnp.dot(normed, wv_ref[...], preferred_element_type=jnp.float32).astype(jnp.bfloat16)


def norm_kv(hidden, gain, wk, wv, cos_full, sin_full):
    rows, width = hidden.shape
    kv_cols = wk.shape[1]
    tile = rows // 2
    row_blk = lambda cols: pl.BlockSpec((tile, cols), lambda i: (i, 0))
    whole = lambda a: pl.BlockSpec(a.shape, lambda i: (0, 0))
    return pl.pallas_call(
        norm_kv_kernel,
        grid=(rows // tile,),
        in_specs=[row_blk(width), whole(gain), whole(wk), whole(wv), row_blk(HEAD), row_blk(HEAD)],
        out_specs=[row_blk(width), row_blk(kv_cols), row_blk(kv_cols)],
        out_shape=[
            jax.ShapeDtypeStruct((rows, width), jnp.bfloat16),
            jax.ShapeDtypeStruct((rows, kv_cols), jnp.bfloat16),
            jax.ShapeDtypeStruct((rows, kv_cols), jnp.bfloat16),
        ],
        compiler_params=pltpu.CompilerParams(dimension_semantics=("arbitrary",), vmem_limit_bytes=VMEM_LIMIT),
        name="norm_kv",
    )(hidden, gain, wk, wv, cos_full, sin_full)


def block_kernel(
    n_tp, n_x, kv_ref, r_ref, posq_ref, cos_ref, sin_ref, wq_ref, wo_ref, hid_ref, out_ref,
    kv, wq, wf, ct, q, mx, ls, acc, hs, ssem, rsem, lsem,
):
    rows, width = r_ref.shape
    heads = wq_ref.shape[1] // HEAD
    kv_heads = mx.shape[1]
    group = heads // kv_heads
    kv_cols = kv_heads * HEAD
    n_chunk, chunk = mx.shape[0], mx.shape[2] // group
    ctx_cols = heads * HEAD
    cols = width // n_tp
    half = rows // 2
    tp, cp = lax.axis_index("tp"), lax.axis_index("cp")
    x, core = cp // 2, cp % 2

    def at_x(dx, dc=0):
        return lax.rem(x + dx + n_x, n_x) * 2 + lax.rem(core + dc, 2)

    def at_y(dy):
        return lax.rem(tp + dy + n_tp, n_tp)

    x_right, x_left, partner = {"cp": at_x(1)}, {"cp": at_x(-1)}, {"cp": at_x(0, 1)}
    y_right, y_left, y_far = {"tp": at_y(1)}, {"tp": at_y(-1)}, {"tp": at_y(2)}

    def rc(src, dst, idx, dev):
        return pltpu.make_async_remote_copy(
            src_ref=src, dst_ref=dst, send_sem=ssem.at[idx], recv_sem=rsem.at[idx], device_id=dev, device_id_type=MESH
        )

    barrier = pltpu.get_barrier_semaphore()
    peers = (x_right, x_left, partner, y_right, y_left, y_far)
    for dev in peers:
        pl.semaphore_signal(barrier, inc=1, device_id=dev, device_id_type=MESH)
    pl.semaphore_wait(barrier, len(peers))

    top, low = pl.ds(0, half), pl.ds(half, half + POS_ROWS)
    kv_copies = [
        rc(kv_ref.at[top], kv.at[2, top], 0, x_right),
        rc(kv_ref.at[low], kv.at[3, low], 1, x_left),
        rc(kv_ref.at[low], kv.at[2, low], 2, x_right),
        rc(kv_ref.at[top], kv.at[3, top], 3, x_left),
        rc(kv_ref, kv.at[1], 4, partner),
        rc(kv.at[2, top], kv.at[6, top], 5, x_right),
        rc(kv.at[3, low], kv.at[6, low], 6, x_left),
        rc(kv.at[2], kv.at[4], 7, partner),
        rc(kv.at[3], kv.at[5], 8, partner),
        rc(kv.at[6], kv.at[7], 9, partner),
    ]
    for cpy in kv_copies[:5]:
        cpy.start()

    piece = wf.shape[1] // (2 * n_x)

    def w_rows(idx, part=None):
        if part is None:
            return pl.ds(pl.multiple_of(idx * piece, piece), piece)
        return pl.ds(pl.multiple_of(idx * piece + part * (piece // 2), piece // 2), piece // 2)

    def w_cols(t):
        return pl.ds(pl.multiple_of(t * cols, cols), cols)

    mine = w_rows(cp)
    w_swap = [
        rc(wo_ref.at[mine, w_cols(at_y(1))], wf.at[1, mine], 10, y_right),
        rc(wo_ref.at[mine, w_cols(at_y(-1))], wf.at[2, mine], 11, y_left),
        rc(wo_ref.at[mine, w_cols(at_y(2))], wf.at[3, mine], 12, y_far),
    ]
    for cpy in w_swap:
        cpy.start()

    n_q = 4
    q_cols = ctx_cols // n_q

    def wq_copy(c):
        sl = pl.ds(pl.multiple_of(c * q_cols, q_cols), q_cols)
        return pltpu.make_async_copy(wq_ref.at[:, sl], wq.at[c], lsem.at[c])

    for c in range(n_q):
        wq_copy(c).start()
    local = [
        pltpu.make_async_copy(kv_ref, kv.at[0], lsem.at[n_q]),
        pltpu.make_async_copy(wo_ref.at[:, w_cols(tp)], wf.at[0], lsem.at[n_q + 1]),
        pltpu.make_async_copy(hid_ref.at[:, w_cols(tp)], hs, lsem.at[n_q + 2]),
    ]
    for cpy in local:
        cpy.start()

    @pl.loop(0, n_q)
    def _(c):
        wq_copy(c).wait()
        qc = jnp.dot(r_ref[...], wq[c], preferred_element_type=jnp.float32)
        per = q_cols // HEAD
        for j in range(per):
            rot = rope(qc[:, j * HEAD : (j + 1) * HEAD], cos_ref[...], sin_ref[...])
            head = c * per + j
            kvh, g = head // group, lax.rem(head, group)
            for i in range(n_chunk):
                q[i, kvh, pl.ds(pl.multiple_of(g * chunk, chunk), chunk), :] = rot[i * chunk : (i + 1) * chunk]

    mx[...] = jnp.full_like(mx, NEG_BIG)
    ls[...] = jnp.zeros_like(ls)
    acc[...] = jnp.zeros_like(acc)
    scale = HEAD**-0.5 * LOG2E

    def attend(i, slot):
        pos_q = posq_ref[pl.ds(pl.multiple_of(i * chunk, chunk), chunk), :]
        hi = kv[slot, pl.ds(rows, 8), :].astype(jnp.float32)
        lo = kv[slot, pl.ds(rows + 8, 8), :].astype(jnp.float32)
        pos_k = (hi * POS_BASE + lo)[0:1, :]
        n_l = rows // HEAD
        bias = jnp.concatenate(
            [jnp.where(pos_k[:, t * HEAD : (t + 1) * HEAD] <= pos_q, 0.0, NEG_BIG) for t in range(n_l)], axis=1
        )
        for kvh in range(kv_heads):
            k_blk = kv[slot, pl.ds(0, rows), kvh * HEAD : (kvh + 1) * HEAD]
            v_blk = kv[slot, pl.ds(0, rows), kv_cols + kvh * HEAD : kv_cols + (kvh + 1) * HEAD]
            s = lax.dot_general(q[i, kvh], k_blk, (((1,), (1,)), ((), ())), preferred_element_type=jnp.float32)
            s = (s.reshape(group, chunk, rows) * scale + bias[None]).reshape(group * chunk, rows)
            m_old = mx[i, kvh]
            m_new = jnp.maximum(m_old, jnp.max(s, axis=1, keepdims=True))
            alpha = jnp.exp2(m_old - m_new)
            p = jnp.exp2(s - jnp.concatenate([m_new] * n_l, axis=1))
            part = p[:, :HEAD]
            for t in range(1, n_l):
                part = part + p[:, t * HEAD : (t + 1) * HEAD]
            mx[i, kvh] = m_new
            ls[i, kvh] = ls[i, kvh] * alpha + part
            acc[i, kvh] = acc[i, kvh] * alpha + jnp.dot(
                p.astype(jnp.bfloat16), v_blk, preferred_element_type=jnp.float32
            )

    def attend_pair(first):
        @pl.loop(0, 2 * n_chunk)
        def _(t):
            attend(t // 2, first + lax.rem(t, 2))

    for cpy in local:
        cpy.wait()
    kv_copies[0].wait_recv()
    kv_copies[5].start()
    kv_copies[1].wait_recv()
    kv_copies[6].start()
    kv_copies[4].wait_recv()
    attend_pair(0)

    for cpy in w_swap:
        cpy.wait_recv()

    def w_piece(idx, part=None):
        return wf.at[pl.ds(1, n_tp - 1), w_rows(idx, part)]

    own, right, left, far = cp, at_x(-1), at_x(1), at_x(2)

    def w_copy(src_idx, idx, dev, part=None):
        return rc(w_piece(src_idx, part), w_piece(src_idx, part), idx, dev)

    kv_copies[2].wait_recv()
    kv_copies[7].start()
    kv_copies[3].wait_recv()
    kv_copies[8].start()
    for idx, dev in ((13, x_right), (14, x_left), (15, partner)):
        w_copy(own, idx, dev).start()
    attend_pair(2)
    kv_copies[5].wait_recv()
    kv_copies[6].wait_recv()
    kv_copies[9].start()
    kv_copies[7].wait_recv()
    kv_copies[8].wait_recv()
    attend_pair(4)
    kv_copies[9].wait_recv()

    base = 24
    hc = chunk // 2

    def rows_of(i, part=None):
        if part is None:
            return pl.ds(pl.multiple_of(i * chunk, chunk), chunk)
        return pl.ds(pl.multiple_of(i * chunk + part * hc, hc), hc)

    def ctx_copies(i):
        sl = rows_of(i)
        first, second = rows_of(i, 0), rows_of(i, 1)
        b = base + 4 * i
        return (
            rc(ct.at[0, sl], ct.at[1, sl], b, y_right),
            rc(ct.at[0, sl], ct.at[2, sl], b + 1, y_left),
            rc(ct.at[1, first], ct.at[3, first], b + 2, y_right),
            rc(ct.at[2, second], ct.at[3, second], b + 3, y_left),
        )

    @pl.loop(0, n_chunk)
    def _(i):
        attend(i, 6)
        attend(i, 7)
        for kvh in range(kv_heads):
            total = jnp.sum(ls[i, kvh], axis=1, keepdims=True)
            ctx = (acc[i, kvh] / total).astype(jnp.bfloat16)
            for g in range(group):
                h = kvh * group + g
                ct[0, rows_of(i), h * HEAD : (h + 1) * HEAD] = ctx[g * chunk : (g + 1) * chunk]
        to_right, to_left, _, _ = ctx_copies(i)
        to_right.start()
        to_left.start()

    def ctx_forward(i):
        to_right, to_left, fwd_right, fwd_left = ctx_copies(i)
        to_right.wait_recv()
        fwd_right.start()
        to_left.wait_recv()
        fwd_left.start()

    ctx_forward(0)
    w_copy(right, 13, x_right).wait_recv()
    w_copy(right, 16, x_right, 0).start()
    w_copy(right, 18, partner).start()
    w_copy(left, 14, x_left).wait_recv()
    w_copy(left, 17, x_left, 1).start()
    w_copy(left, 19, partner).start()
    ctx_forward(1)
    ctx_forward(2)
    w_copy(far, 16, x_right, 0).wait_recv()
    w_copy(far, 17, x_left, 1).wait_recv()
    w_copy(far, 20, partner).start()
    ctx_forward(3)
    for idx, src in ((15, own), (18, right), (19, left), (20, far)):
        w_copy(src, idx, partner).wait_recv()

    out_base = base + 4 * n_chunk

    def out_copies(i):
        sl, first, second = rows_of(i), rows_of(i, 0), rows_of(i, 1)
        b = out_base + 4 * i
        mine_c, right_c, left_c = w_cols(tp), w_cols(at_y(-1)), w_cols(at_y(1))
        return (
            rc(out_ref.at[sl, mine_c], out_ref.at[sl, mine_c], b, y_right),
            rc(out_ref.at[sl, mine_c], out_ref.at[sl, mine_c], b + 1, y_left),
            rc(out_ref.at[first, right_c], out_ref.at[first, right_c], b + 2, y_right),
            rc(out_ref.at[second, left_c], out_ref.at[second, left_c], b + 3, y_left),
        )

    @pl.loop(0, n_chunk)
    def _(i):
        _, _, fwd_right, fwd_left = ctx_copies(i)
        fwd_right.wait_recv()
        fwd_left.wait_recv()
        sl = rows_of(i)
        y = hs[sl, :].astype(jnp.float32)
        proj = jnp.dot(ct[0, sl, :], wf[0], preferred_element_type=jnp.float32)
        for j in range(1, n_tp):
            proj = proj + jnp.dot(ct[j, sl, :], wf[j], preferred_element_type=jnp.float32)
        out_ref[sl, w_cols(tp)] = (y + proj).astype(jnp.bfloat16)
        to_right, to_left, _, _ = out_copies(i)
        to_right.start()
        to_left.start()

    @pl.loop(0, n_chunk)
    def _(i):
        to_right, to_left, fwd_right, fwd_left = out_copies(i)
        to_right.wait_recv()
        fwd_right.start()
        to_left.wait_recv()
        fwd_left.start()

    for cpy in kv_copies + w_swap:
        cpy.wait_send()
    for src, idx, dev, part in (
        (own, 13, x_right, None), (own, 14, x_left, None), (own, 15, partner, None), (right, 16, x_right, 0),
        (left, 17, x_left, 1), (right, 18, partner, None), (left, 19, partner, None), (far, 20, partner, None),
    ):
        w_copy(src, idx, dev, part).wait_send()

    @pl.loop(0, n_chunk)
    def _(i):
        for cpy in ctx_copies(i):
            cpy.wait_send()
        for cpy in out_copies(i):
            cpy.wait_send()
        _, _, fwd_right, fwd_left = out_copies(i)
        fwd_right.wait_recv()
        fwd_left.wait_recv()


def attention_block(mesh, kv_blk, normed, pos_q, cos_full, sin_full, w_query, w_out, hidden):
    n_tp, n_x = mesh.shape["tp"], mesh.shape["cp"] // 2
    rows, width = hidden.shape
    heads = w_query.shape[1] // HEAD
    kv_heads = kv_blk.shape[1] // (2 * HEAD)
    n_chunk = 4
    chunk = rows // n_chunk
    grp = heads // kv_heads * chunk
    bf16, f32 = jnp.bfloat16, jnp.float32
    n_sem = 24 + 8 * n_chunk
    return pl.pallas_call(
        functools.partial(block_kernel, n_tp, n_x),
        out_shape=jax.ShapeDtypeStruct((rows, width), bf16),
        in_specs=[vmem_spec()] * 5 + [any_spec()] * 3,
        out_specs=vmem_spec(),
        scratch_shapes=[
            pltpu.VMEM((2 * n_x, *kv_blk.shape), bf16),
            pltpu.VMEM((4, width, w_query.shape[1] // 4), bf16),
            pltpu.VMEM((n_tp, w_out.shape[0], width // n_tp), bf16),
            pltpu.VMEM((n_tp, rows, heads * HEAD), bf16),
            pltpu.VMEM((n_chunk, kv_heads, grp, HEAD), bf16),
            pltpu.VMEM((n_chunk, kv_heads, grp, HEAD), f32),
            pltpu.VMEM((n_chunk, kv_heads, grp, HEAD), f32),
            pltpu.VMEM((n_chunk, kv_heads, grp, HEAD), f32),
            pltpu.VMEM((rows, width // n_tp), bf16),
            pltpu.SemaphoreType.DMA((n_sem,)),
            pltpu.SemaphoreType.DMA((n_sem,)),
            pltpu.SemaphoreType.DMA((8,)),
        ],
        compiler_params=pltpu.CompilerParams(collective_id=0, has_side_effects=True, vmem_limit_bytes=VMEM_LIMIT),
        name="attention_block",
    )(kv_blk, normed, pos_q, cos_full, sin_full, w_query, w_out, hidden)


def solution(mesh):
    def local_block(hidden, tok_pos, norm_gain, w_query, w_key, w_value, w_out):
        rows = hidden.shape[0]
        kv_loc = w_key.shape[1] // HEAD
        cos_full, sin_full = rope_tables(tok_pos)
        normed, k_rot, values = norm_kv(hidden, norm_gain[None, :], w_key, w_value, cos_full, sin_full)
        pos_cols = jnp.stack([tok_pos // POS_BASE, tok_pos % POS_BASE]).astype(jnp.bfloat16)
        pos_rows = jnp.repeat(pos_cols, POS_ROWS // 2, axis=0)
        kv_blk = jnp.concatenate([jnp.concatenate([k_rot, values], axis=1), pos_rows], axis=0)
        pos_q = jnp.broadcast_to(tok_pos.astype(jnp.float32)[:, None], (rows, HEAD))
        hidden_out = attention_block(mesh, kv_blk, normed, pos_q, cos_full, sin_full, w_query, w_out, hidden)
        return hidden_out, k_rot.reshape(rows, kv_loc, HEAD), values.reshape(rows, kv_loc, HEAD)

    row_spec = P(("dp", "cp"), None)
    cache_spec = P(("dp", "cp"), "tp", None)
    return jax.shard_map(
        local_block,
        mesh=mesh,
        in_specs=(row_spec, P(("dp", "cp")), P(None), P(None, "tp"), P(None, "tp"), P(None, "tp"), P("tp", None)),
        out_specs=(row_spec, cache_spec, cache_spec),
        check_vma=False,
    )
```

time: 333 us -> 137 us (0.41)
  waiting for transfers between devices: 179 us -> 0 us
  Pallas kernels: 0 us -> 122 us
  matrix products: 66.6 us -> 0 us
  other arithmetic: 31.2 us -> 4.7 us
  starting transfers between devices: 24.4 us -> 0 us
  between operations: 14.3 us -> 0.67 us
  local copies, waits for them, and re-layouts: 16.4 us -> 9.57 us
    psum x1 -> x0, waiting for transfers between devices: 158 us -> none  [local_block(): attn_proj = lax.psum(part_proj, 'tp')]
    pallas_call x0 -> x2, Pallas kernels: none -> 122 us  [the longest x1 115 us: attention_block(): pl.pallas_call(functools.partial(block_kernel, n_tp, n_x), out_shape=jax....]
    dot_general x20 -> x0, matrix products: 66.6 us -> none  [the longest x8 26.3 us: absorb(): jnp.einsum('kgqt,tkd->kgqd', exp_scores.astype(jnp.bfloat16), v_blk, pref...]
    ppermute x21 -> x0, starting transfers between devices: 24.3 us -> none  [the longest x7 12.6 us: step(): k_blk = lax.ppermute(k_blk, 'cp', shift_pairs)]
    ppermute x21 -> x0, waiting for transfers between devices: 21 us -> none  [the longest x7 21 us: step(): pos_blk = lax.ppermute(pos_blk, 'cp', shift_pairs)]
    reduce_sum x9 -> x0, other arithmetic: 17.3 us -> none  [the longest x8 14.2 us: absorb(): row_sum = row_sum * rescale + jnp.sum(exp_scores, axis=-1)]
    while x57 -> x0, local copies, waits for them, and re-layouts: 10.4 us -> none
    convert_element_type x1 -> x0, other arithmetic: 8 us -> none  [local_block(): hidden_out = (hid_f32 + attn_proj).astype(jnp.bfloat16)]
  transfers between devices with their start and end apart: 22 -> 0, of which waited for: 8 -> 0; matrix products, arithmetic and copies ran while one was open for 8% -> 0% of each run, Pallas kernels for 0% -> 0%
where the time goes in v1:
time: 137 us
  Pallas kernels  122 us (89%)
  local copies, waits for them, and re-layouts  9.57 us (7%)
  other arithmetic  4.7 us (3%)
    pallas_call x1, Pallas kernels, attention_block(): pl.pallas_call(functools.partial(block_kernel, n_tp, n_x), out_shape=jax....  115 us
    pallas_call x1, Pallas kernels, norm_kv(): pl.pallas_call(norm_kv_kernel, grid=(rows // tile,), in_specs=[row_blk(wi...  7.48 us
    unnamed x1, local copies, waits for them, and re-layouts  4.7 us

profile of v1, /device:TPU:97, one launch (start us, length us, event | category | flops | bytes accessed | tf_op | source)
XLA Modules:
  0.0 136.9 jit_solution(14535227115292030456)
XLA Ops:
  0.6 0.8 fusion.4
  1.5 0.6 broadcast_bitcast_fusion
  2.1 0.8 broadcast_in_dim.16.posq_ref
  2.9 1.0 fusion
  3.9 1.0 pad_maximum_fusion.1
  4.9 7.5 %norm_kv.1 = (bf16[512,4096]{1,0:T(8,128)(2,1)}, bf16[512,256]{1,0:T(8,128)(2,1)}, bf16[512,256]{1,0:T(8,128)(2,1)}) custom-call(bf16[512,4096]{1,0:T(8,128)(2,1)} %hid_ref.3, f32[1,4096]{1,0:T(1,128)} %bitcast.3, bf16[4096,256]{1,0:T(8,128)(2,1)} %wk_ref.1, bf16[4096,256]{1,0:T(8,128)(2,1)} %wv_ref.1, f32[512,128]{1,0:T(8,128)} %get-tuple-element.15.cos_ref, ...), custom_call_target="tpu_custom_call" | custom-call | tf_op jit(solution)/shard_map/norm_kv/pallas_call | solution.py:59
  12.4 1.7 %reshape.23 = bf16[512,2,128]{2,1,0:T(2,128)(2,1)} reshape(bf16[512,256]{1,0:T(8,128)(2,1)} %get-tuple-element.6) | data formatting | bytes 524288 | tf_op jit(solution)/shard_map/reshape | solution.py:402
  14.1 1.9 %pad_maximum_fusion.kv_ref = bf16[528,512]{1,0:T(8,128)(2,1)} fusion(bf16[16,512]{1,0:T(8,128)(2,1)} %broadcast_bitcast_fusion, bf16[512,256]{1,0:T(8,128)(2,1)} %get-tuple-element.7, bf16[512,256]{1,0:T(8,128)(2,1)} %get-tuple-element.6), kind=kLoop, calls=%fused_computation | loop fusion | flops 1622016 | bytes 1081344 | tf_op jit(solution)/shard_map/concatenate | solution.py:399
  16.0 114.5 %attention_block.1 = bf16[512,4096]{1,0:T(8,128)(2,1)} custom-call(bf16[528,512]{1,0:T(8,128)(2,1)} %pad_maximum_fusion.kv_ref, bf16[512,4096]{1,0:T(8,128)(2,1)} %get-tuple-element.8.r_ref, f32[512,128]{1,0:T(8,128)} %broadcast_in_dim.16.posq_ref, f32[512,128]{1,0:T(8,128)} %get-tuple-element.15.cos_ref, f32[512,128]{1,0:T(8,128)} %get-tuple-element.16.sin_ref, ...), custom_call_target="tpu_custom_call" | custom-call | tf_op jit(solution)/shard_map/attention_block/pallas_call | solution.py:367
  130.5 1.7 %reshape.24 = bf16[512,2,128]{2,1,0:T(2,128)(2,1)} reshape(bf16[512,256]{1,0:T(8,128)(2,1)} %get-tuple-element.7) | data formatting | bytes 524288 | tf_op jit(solution)/shard_map/reshape | solution.py:402
  132.2 4.7 %copy.11 = bf16[512,4096]{1,0:T(8,128)(2,1)} copy(bf16[512,4096]{1,0:T(8,128)(2,1)} %attention_block.1) | data formatting | bytes 8388608
  (4 shorter events, 0.0 us)

commit v2 on v1

--- a/solution.py
+++ b/solution.py
@@ -26,11 +26,9 @@
     return pl.BlockSpec(memory_space=pl.ANY)
 
 
-def rope_tables(tok_pos):
-    inv_freq = 1.0 / (THETA ** (jnp.arange(0, HEAD, 2, dtype=jnp.float32) / HEAD))
-    angles = tok_pos.astype(jnp.float32)[:, None] * inv_freq[None, :]
-    cos, sin = jnp.cos(angles), jnp.sin(angles)
-    return jnp.concatenate([cos, cos], axis=-1), jnp.concatenate([-sin, sin], axis=-1)
+def inv_freq_row():
+    freq = 1.0 / (THETA ** (jnp.arange(0, HEAD, 2, dtype=jnp.float32) / HEAD))
+    return jnp.concatenate([freq, freq])[None, :]
 
 
 def rope(head_f32, cos_full, sin_full):
@@ -38,42 +36,139 @@
     return (vals * cos_full + pltpu.roll(vals, HEAD // 2, 1) * sin_full).astype(jnp.bfloat16)
 
 
-def norm_kv_kernel(hid_ref, gain_ref, wk_ref, wv_ref, cos_ref, sin_ref, r_ref, k_ref, v_ref):
-    x = hid_ref[...].astype(jnp.float32)
-    scaled = x * lax.rsqrt(jnp.mean(x * x, axis=-1, keepdims=True) + EPS)
-    normed = (scaled * gain_ref[...]).astype(jnp.bfloat16)
-    r_ref[...] = normed
-    k = jnp.dot(normed, wk_ref[...], preferred_element_type=jnp.float32)
-    for h in range(k.shape[1] // HEAD):
-        cols = slice(h * HEAD, (h + 1) * HEAD)
-        k_ref[:, cols] = rope(k[:, cols], cos_ref[...], sin_ref[...])
-    v_ref[...] = jnp.dot(normed, wv_ref[...], preferred_element_type=jnp.float32).astype(jnp.bfloat16)
-
-
-def norm_kv(hidden, gain, wk, wv, cos_full, sin_full):
+def position_columns(pos_row):
+    tiles = []
+    for t in range(pos_row.shape[1] // HEAD):
+        tile = jnp.broadcast_to(pos_row[:, t * HEAD : (t + 1) * HEAD], (HEAD, HEAD))
+        tiles.append(jnp.transpose(tile))
+    return jnp.concatenate(tiles, axis=0)
+
+
+def norm_kv_kernel(
+    pos_ref, freq_ref, gain_ref, hid_ref, wk_ref, wv_ref, r_out, kv_ref, cos_ref, sin_ref, kc_ref, vc_ref,
+    hid, wk, wv, r, lsem,
+):
+    rows = hid.shape[0]
+    kv_cols = wk.shape[1]
+    n_part = 2
+    part = rows // n_part
+
+    def hid_copy(i):
+        sl = slice(i * part, (i + 1) * part)
+        return pltpu.make_async_copy(hid_ref.at[sl], hid.at[sl], lsem.at[i])
+
+    def r_copy(i):
+        sl = slice(i * part, (i + 1) * part)
+        return pltpu.make_async_copy(r.at[sl], r_out.at[sl], lsem.at[n_part + i])
+
+    w_copies = [
+        pltpu.make_async_copy(wk_ref, wk, lsem.at[2 * n_part]),
+        pltpu.make_async_copy(wv_ref, wv, lsem.at[2 * n_part + 1]),
+    ]
+    for i in range(n_part):
+        hid_copy(i).start()
+    for cpy in w_copies:
+        cpy.start()
+
+    pos = pos_ref[...]
+    pos_row = jnp.concatenate([pos[t : t + 1] for t in range(pos.shape[0])], axis=1)
+    angles = position_columns(pos_row.astype(jnp.float32)) * freq_ref[...]
+    lane = lax.broadcasted_iota(jnp.int32, angles.shape, 1)
+    sines = jnp.sin(angles)
+    cos_ref[...] = jnp.cos(angles)
+    sin_ref[...] = jnp.where(lane < HEAD // 2, -sines, sines)
+    hi = jnp.broadcast_to((pos_row // POS_BASE).astype(jnp.float32), (POS_ROWS // 2, rows))
+    lo = jnp.broadcast_to(lax.rem(pos_row, POS_BASE).astype(jnp.float32), (POS_ROWS // 2, rows))
+    kv_ref[rows:, :] = jnp.concatenate([hi, lo], axis=0).astype(jnp.bfloat16)
+
+    for i in range(n_part):
+        sl = slice(i * part, (i + 1) * part)
+        hid_copy(i).wait()
+        x = hid[sl, :].astype(jnp.float32)
+        scaled = x * lax.rsqrt(jnp.mean(x * x, axis=-1, keepdims=True) + EPS)
+        r[sl, :] = (scaled * gain_ref[...]).astype(jnp.bfloat16)
+        r_copy(i).start()
+        if i == 0:
+            for cpy in w_copies:
+                cpy.wait()
+        k = jnp.dot(r[sl, :], wk[...], preferred_element_type=jnp.float32)
+        v = jnp.dot(r[sl, :], wv[...], preferred_element_type=jnp.float32).astype(jnp.bfloat16)
+        kv_ref[sl, kv_cols:] = v
+        rots = []
+        for h in range(kv_cols // HEAD):
+            cols = slice(h * HEAD, (h + 1) * HEAD)
+            rot = rope(k[:, cols], cos_ref[sl, :], sin_ref[sl, :])
+            kv_ref[sl, cols] = rot
+            rots.append(rot)
+        kc_ref[sl] = jnp.stack(rots, axis=1)
+        vc_ref[sl] = jnp.stack([v[:, h * HEAD : (h + 1) * HEAD] for h in range(kv_cols // HEAD)], axis=1)
+    for i in range(n_part):
+        r_copy(i).wait()
+
+
+def norm_kv(pos, freq, gain, hidden, wk, wv):
     rows, width = hidden.shape
     kv_cols = wk.shape[1]
-    tile = rows // 2
-    row_blk = lambda cols: pl.BlockSpec((tile, cols), lambda i: (i, 0))
-    whole = lambda a: pl.BlockSpec(a.shape, lambda i: (0, 0))
+    bf16, f32 = jnp.bfloat16, jnp.float32
+    cache = jax.ShapeDtypeStruct((rows, kv_cols // HEAD, HEAD), bf16)
+    table = jax.ShapeDtypeStruct((rows, HEAD), f32)
     return pl.pallas_call(
         norm_kv_kernel,
-        grid=(rows // tile,),
-        in_specs=[row_blk(width), whole(gain), whole(wk), whole(wv), row_blk(HEAD), row_blk(HEAD)],
-        out_specs=[row_blk(width), row_blk(kv_cols), row_blk(kv_cols)],
+        in_specs=[vmem_spec()] * 3 + [any_spec()] * 3,
+        out_specs=[any_spec()] + [vmem_spec()] * 5,
         out_shape=[
-            jax.ShapeDtypeStruct((rows, width), jnp.bfloat16),
-            jax.ShapeDtypeStruct((rows, kv_cols), jnp.bfloat16),
-            jax.ShapeDtypeStruct((rows, kv_cols), jnp.bfloat16),
+            jax.ShapeDtypeStruct((rows, width), bf16),
+            jax.ShapeDtypeStruct((rows + POS_ROWS, 2 * kv_cols), bf16),
+            table, table, cache, cache,
         ],
-        compiler_params=pltpu.CompilerParams(dimension_semantics=("arbitrary",), vmem_limit_bytes=VMEM_LIMIT),
+        scratch_shapes=[
+            pltpu.VMEM((rows, width), bf16),
+            pltpu.VMEM(wk.shape, bf16),
+            pltpu.VMEM(wv.shape, bf16),
+            pltpu.VMEM((rows, width), bf16),
+            pltpu.SemaphoreType.DMA((8,)),
+        ],
+        compiler_params=pltpu.CompilerParams(vmem_limit_bytes=VMEM_LIMIT),
         name="norm_kv",
-    )(hidden, gain, wk, wv, cos_full, sin_full)
+    )(pos, freq, gain, hidden, wk, wv)
+
+
+def copy_kernel(src, dst, buf, isem, osem):
+    n = buf.shape[0]
+    tile = src.shape[0] // n
+    def load(i):
+        return pltpu.make_async_copy(src.at[pl.ds(i * tile, tile)], buf.at[i], isem.at[i])
+    def store(i):
+        return pltpu.make_async_copy(buf.at[i], dst.at[pl.ds(i * tile, tile)], osem.at[i])
+    for i in range(n):
+        load(i).start()
+    for i in range(n):
+        load(i).wait()
+        store(i).start()
+    for i in range(n):
+        store(i).wait()
+
+
+def copy_out(arr):
+    n = 8
+    rows, width = arr.shape
+    return pl.pallas_call(
+        copy_kernel,
+        in_specs=[any_spec()],
+        out_specs=any_spec(),
+        out_shape=jax.ShapeDtypeStruct(arr.shape, arr.dtype),
+        scratch_shapes=[
+            pltpu.VMEM((n, rows // n, width), arr.dtype),
+            pltpu.SemaphoreType.DMA((n,)),
+            pltpu.SemaphoreType.DMA((n,)),
+        ],
+        name="copy_out",
+    )(arr)
 
 
 def block_kernel(
-    n_tp, n_x, kv_ref, r_ref, posq_ref, cos_ref, sin_ref, wq_ref, wo_ref, hid_ref, out_ref,
-    kv, wq, wf, ct, q, mx, ls, acc, hs, ssem, rsem, lsem,
+    n_tp, n_x, kv_ref, r_hbm, cos_hbm, sin_hbm, wq_ref, wo_ref, hid_ref, out_hbm,
+    kv, r_ref, cos_ref, sin_ref, wq, wf, ct, q, mx, ls, acc, hs, pos_q_ref, out_ref, ssem, rsem, lsem,
 ):
     rows, width = r_ref.shape
     heads = wq_ref.shape[1] // HEAD
@@ -149,15 +244,22 @@
         sl = pl.ds(pl.multiple_of(c * q_cols, q_cols), q_cols)
         return pltpu.make_async_copy(wq_ref.at[:, sl], wq.at[c], lsem.at[c])
 
+    local = [
+        pltpu.make_async_copy(cos_hbm, cos_ref, lsem.at[n_q]),
+        pltpu.make_async_copy(sin_hbm, sin_ref, lsem.at[n_q + 1]),
+        pltpu.make_async_copy(r_hbm, r_ref, lsem.at[n_q + 2]),
+        pltpu.make_async_copy(kv_ref, kv.at[0], lsem.at[n_q + 3]),
+        pltpu.make_async_copy(wo_ref.at[:, w_cols(tp)], wf.at[0], lsem.at[n_q + 4]),
+        pltpu.make_async_copy(hid_ref.at[:, w_cols(tp)], hs, lsem.at[n_q + 5]),
+    ]
+    for cpy in local[:3]:
+        cpy.start()
     for c in range(n_q):
         wq_copy(c).start()
-    local = [
-        pltpu.make_async_copy(kv_ref, kv.at[0], lsem.at[n_q]),
-        pltpu.make_async_copy(wo_ref.at[:, w_cols(tp)], wf.at[0], lsem.at[n_q + 1]),
-        pltpu.make_async_copy(hid_ref.at[:, w_cols(tp)], hs, lsem.at[n_q + 2]),
-    ]
-    for cpy in local:
+    for cpy in local[3:]:
         cpy.start()
+    for cpy in local[:3]:
+        cpy.wait()
 
     @pl.loop(0, n_q)
     def _(c):
@@ -176,11 +278,14 @@
     acc[...] = jnp.zeros_like(acc)
     scale = HEAD**-0.5 * LOG2E
 
+    def block_positions(slot):
+        hi = kv[slot, pl.ds(rows, POS_ROWS // 2), :].astype(jnp.float32)
+        lo = kv[slot, pl.ds(rows + POS_ROWS // 2, POS_ROWS // 2), :].astype(jnp.float32)
+        return (hi * POS_BASE + lo)[0:1, :]
+
     def attend(i, slot):
-        pos_q = posq_ref[pl.ds(pl.multiple_of(i * chunk, chunk), chunk), :]
-        hi = kv[slot, pl.ds(rows, 8), :].astype(jnp.float32)
-        lo = kv[slot, pl.ds(rows + 8, 8), :].astype(jnp.float32)
-        pos_k = (hi * POS_BASE + lo)[0:1, :]
+        pos_q = pos_q_ref[pl.ds(pl.multiple_of(i * chunk, chunk), chunk), :]
+        pos_k = block_positions(slot)
         n_l = rows // HEAD
         bias = jnp.concatenate(
             [jnp.where(pos_k[:, t * HEAD : (t + 1) * HEAD] <= pos_q, 0.0, NEG_BIG) for t in range(n_l)], axis=1
@@ -203,13 +308,16 @@
                 p.astype(jnp.bfloat16), v_blk, preferred_element_type=jnp.float32
             )
 
+    n_lead = n_chunk // 2
+
     def attend_pair(first):
-        @pl.loop(0, 2 * n_chunk)
+        @pl.loop(0, 2 * n_lead)
         def _(t):
             attend(t // 2, first + lax.rem(t, 2))
 
-    for cpy in local:
+    for cpy in local[3:]:
         cpy.wait()
+    pos_q_ref[...] = position_columns(block_positions(0))
     kv_copies[0].wait_recv()
     kv_copies[5].start()
     kv_copies[1].wait_recv()
@@ -262,10 +370,7 @@
             rc(ct.at[2, second], ct.at[3, second], b + 3, y_left),
         )
 
-    @pl.loop(0, n_chunk)
-    def _(i):
-        attend(i, 6)
-        attend(i, 7)
+    def finish(i):
         for kvh in range(kv_heads):
             total = jnp.sum(ls[i, kvh], axis=1, keepdims=True)
             ctx = (acc[i, kvh] / total).astype(jnp.bfloat16)
@@ -283,14 +388,27 @@
         to_left.wait_recv()
         fwd_left.start()
 
-    ctx_forward(0)
+    @pl.loop(0, n_lead)
+    def _(i):
+        attend(i, 6)
+        attend(i, 7)
+        finish(i)
+
+    @pl.loop(n_lead, n_chunk)
+    def _(i):
+        @pl.loop(0, 2 * n_x)
+        def _(slot):
+            attend(i, slot)
+
+        finish(i)
+        ctx_forward(i - n_lead)
+
     w_copy(right, 13, x_right).wait_recv()
     w_copy(right, 16, x_right, 0).start()
     w_copy(right, 18, partner).start()
     w_copy(left, 14, x_left).wait_recv()
     w_copy(left, 17, x_left, 1).start()
     w_copy(left, 19, partner).start()
-    ctx_forward(1)
     ctx_forward(2)
     w_copy(far, 16, x_right, 0).wait_recv()
     w_copy(far, 17, x_left, 1).wait_recv()
@@ -335,6 +453,9 @@
         to_left.wait_recv()
         fwd_left.start()
 
+    def out_store(i):
+        return pltpu.make_async_copy(out_ref.at[rows_of(i)], out_hbm.at[rows_of(i)], lsem.at[i])
+
     for cpy in kv_copies + w_swap:
         cpy.wait_send()
     for src, idx, dev, part in (
@@ -352,9 +473,14 @@
         _, _, fwd_right, fwd_left = out_copies(i)
         fwd_right.wait_recv()
         fwd_left.wait_recv()
-
-
-def attention_block(mesh, kv_blk, normed, pos_q, cos_full, sin_full, w_query, w_out, hidden):
+        out_store(i).start()
+
+    @pl.loop(0, n_chunk)
+    def _(i):
+        out_store(i).wait()
+
+
+def attention_block(mesh, kv_blk, normed, cos_full, sin_full, w_query, w_out, hidden):
     n_tp, n_x = mesh.shape["tp"], mesh.shape["cp"] // 2
     rows, width = hidden.shape
     heads = w_query.shape[1] // HEAD
@@ -367,10 +493,13 @@
     return pl.pallas_call(
         functools.partial(block_kernel, n_tp, n_x),
         out_shape=jax.ShapeDtypeStruct((rows, width), bf16),
-        in_specs=[vmem_spec()] * 5 + [any_spec()] * 3,
-        out_specs=vmem_spec(),
+        in_specs=[any_spec()] * 7,
+        out_specs=any_spec(),
         scratch_shapes=[
             pltpu.VMEM((2 * n_x, *kv_blk.shape), bf16),
+            pltpu.VMEM((rows, width), bf16),
+            pltpu.VMEM((rows, HEAD), f32),
+            pltpu.VMEM((rows, HEAD), f32),
             pltpu.VMEM((4, width, w_query.shape[1] // 4), bf16),
             pltpu.VMEM((n_tp, w_out.shape[0], width // n_tp), bf16),
             pltpu.VMEM((n_tp, rows, heads * HEAD), bf16),
@@ -379,27 +508,24 @@
             pltpu.VMEM((n_chunk, kv_heads, grp, HEAD), f32),
             pltpu.VMEM((n_chunk, kv_heads, grp, HEAD), f32),
             pltpu.VMEM((rows, width // n_tp), bf16),
+            pltpu.VMEM((rows, HEAD), f32),
+            pltpu.VMEM((rows, width), bf16),
             pltpu.SemaphoreType.DMA((n_sem,)),
             pltpu.SemaphoreType.DMA((n_sem,)),
-            pltpu.SemaphoreType.DMA((8,)),
+            pltpu.SemaphoreType.DMA((16,)),
         ],
         compiler_params=pltpu.CompilerParams(collective_id=0, has_side_effects=True, vmem_limit_bytes=VMEM_LIMIT),
         name="attention_block",
-    )(kv_blk, normed, pos_q, cos_full, sin_full, w_query, w_out, hidden)
+    )(kv_blk, normed, cos_full, sin_full, w_query, w_out, hidden)
 
 
 def solution(mesh):
     def local_block(hidden, tok_pos, norm_gain, w_query, w_key, w_value, w_out):
-        rows = hidden.shape[0]
-        kv_loc = w_key.shape[1] // HEAD
-        cos_full, sin_full = rope_tables(tok_pos)
-        normed, k_rot, values = norm_kv(hidden, norm_gain[None, :], w_key, w_value, cos_full, sin_full)
-        pos_cols = jnp.stack([tok_pos // POS_BASE, tok_pos % POS_BASE]).astype(jnp.bfloat16)
-        pos_rows = jnp.repeat(pos_cols, POS_ROWS // 2, axis=0)
-        kv_blk = jnp.concatenate([jnp.concatenate([k_rot, values], axis=1), pos_rows], axis=0)
-        pos_q = jnp.broadcast_to(tok_pos.astype(jnp.float32)[:, None], (rows, HEAD))
-        hidden_out = attention_block(mesh, kv_blk, normed, pos_q, cos_full, sin_full, w_query, w_out, hidden)
-        return hidden_out, k_rot.reshape(rows, kv_loc, HEAD), values.reshape(rows, kv_loc, HEAD)
+        normed, kv_blk, cos_full, sin_full, k_cache, v_cache = norm_kv(
+            tok_pos.reshape(-1, HEAD), inv_freq_row(), norm_gain[None, :], hidden, w_key, w_value
+        )
+        hidden_out = attention_block(mesh, kv_blk, normed, cos_full, sin_full, w_query, w_out, hidden)
+        return copy_out(hidden_out), k_cache, v_cache
 
     row_spec = P(("dp", "cp"), None)
     cache_spec = P(("dp", "cp"), "tp", None)

time: 137 us -> 118 us (0.86)
  local copies, waits for them, and re-layouts: 9.57 us -> 0 us
  Pallas kernels: 122 us -> 116 us
  other arithmetic: 4.7 us -> 0.59 us
    pallas_call x1, Pallas kernels: 115 us -> 103 us  [attention_block(): pl.pallas_call(functools.partial(block_kernel, n_tp, n_x), out_shape=jax....]
    pallas_call x1 -> x2, Pallas kernels: 7.48 us -> 13.2 us  [the longest x1 9.67 us: norm_kv(): pl.pallas_call(norm_kv_kernel, in_specs=[vmem_spec()] * 3 + [any_spec()]...]
    unnamed x1 -> x0, local copies, waits for them, and re-layouts: 4.7 us -> none
    reshape x3 -> x0, local copies, waits for them, and re-layouts: 4.04 us -> none  [the longest x1 1.72 us: local_block(): values.reshape(rows, kv_loc, HEAD)]
    concatenate x2 -> x0, other arithmetic: 2.92 us -> none  [the longest x1 1.9 us: local_block(): jnp.concatenate([jnp.concatenate([k_rot, values], axis=1), pos_rows], axi...]
where the time goes in v2:
time: 118 us; the launch traced here: 117 us
  Pallas kernels  116 us (98%)
    pallas_call x1, Pallas kernels, attention_block(): pl.pallas_call(functools.partial(block_kernel, n_tp, n_x), out_shape=jax....  103 us
    pallas_call x1, Pallas kernels, norm_kv(): pl.pallas_call(norm_kv_kernel, in_specs=[vmem_spec()] * 3 + [any_spec()]...  9.67 us
    pallas_call x1, Pallas kernels, copy_out(): pl.pallas_call(copy_kernel, in_specs=[any_spec()], out_specs=any_spec(),...  3.58 us

profile of v2, /device:TPU:97, one launch (start us, length us, event | category | flops | bytes accessed | tf_op | source)
XLA Modules:
  0.0 117.5 jit_solution(17785138290248693329)
XLA Ops:
  0.6 0.6 maximum_bitcast_fusion.freq_ref
  1.2 9.7 %norm_kv.1 = (bf16[512,4096]{1,0:T(8,128)(2,1)}, bf16[528,512]{1,0:T(8,128)(2,1)}, f32[512,128]{1,0:T(8,128)}, f32[512,128]{1,0:T(8,128)}, bf16[512,2,128]{2,1,0:T(2,128)(2,1)}, /*index=5*/bf16[512,2,128]{2,1,0:T(2,128)(2,1)}) custom-call(s32[4,128]{1,0:T(4,128)} %bitcast.5, f32[1,128]{1,0:T(1,128)} %maximum_bitcast_fusion.freq_ref, f32[1,4096]{1,0:T(1,128)} %bitcast.4, ...), custom_call_target="tpu_custom_call" | custom-call | tf_op jit(solution)/shard_map/norm_kv/pallas_call | solution.py:115
  10.9 102.8 %attention_block.1.src = bf16[512,4096]{1,0:T(8,128)(2,1)} custom-call(bf16[528,512]{1,0:T(8,128)(2,1)} %get-tuple-element.9.kv_ref, bf16[512,4096]{1,0:T(8,128)(2,1)} %get-tuple-element.10.r_hbm, f32[512,128]{1,0:T(8,128)} %get-tuple-element.11.cos_hbm, f32[512,128]{1,0:T(8,128)} %get-tuple-element.12.sin_hbm, bf16[4096,1024]{1,0:T(8,128)(2,1)} %wq_ref.1, ...), custom_call_target="tpu_custom_call" | custom-call | tf_op jit(solution)/shard_map/attention_block/pallas_call | solution.py:493
  113.8 3.6 %copy_out.1 = bf16[512,4096]{1,0:T(8,128)(2,1)} custom-call(bf16[512,4096]{1,0:T(8,128)(2,1)} %attention_block.1.src), custom_call_target="tpu_custom_call" | custom-call | tf_op jit(solution)/shard_map/copy_out/pallas_call | solution.py:155
  (1 shorter events, 0.0 us)

commit v3 on v0

v3 whole, which is shorter than its diff:
```python
import functools

import jax
import jax.numpy as jnp
from jax import lax
from jax.experimental import pallas as pl
from jax.experimental.pallas import tpu as pltpu
from jax.sharding import PartitionSpec as P

HEAD = 128
THETA = 1000000
EPS = 1e-5
NEG_BIG = -1e30
LOG2E = 1.4426950408889634
MESH = pl.DeviceIdType.MESH
VMEM_LIMIT = 64 * 2**20 - 64 * 2**10
POS_ROWS = 16
POS_BASE = 64
E_FRACTION = (3, 8)
N_Q = 4


def vmem_spec():
    return pl.BlockSpec(memory_space=pltpu.VMEM)


def any_spec():
    return pl.BlockSpec(memory_space=pl.ANY)


def inv_freq_row():
    freq = 1.0 / (THETA ** (jnp.arange(0, HEAD, 2, dtype=jnp.float32) / HEAD))
    return jnp.concatenate([freq, freq])[None, :]


def rope(head_f32, cos_full, sin_full):
    vals = head_f32.astype(jnp.bfloat16).astype(jnp.float32)
    return (vals * cos_full + pltpu.roll(vals, HEAD // 2, 1) * sin_full).astype(jnp.bfloat16)


def position_columns(pos_row):
    tiles = []
    for t in range(pos_row.shape[1] // HEAD):
        tile = jnp.broadcast_to(pos_row[:, t * HEAD : (t + 1) * HEAD], (HEAD, HEAD))
        tiles.append(jnp.transpose(tile))
    return jnp.concatenate(tiles, axis=0)


def block_kernel(
    n_tp, n_x, pos_ref, freq_ref, gain_ref, hid_hbm, wk_hbm, wv_hbm, wq_hbm, wo_hbm, out_hbm, kc_hbm, vc_hbm,
    kv, r, cos, sin, wq, wr, we, ct, q, mx, ls, acc, acc_e, pos_q, out, kc, vc, ssem, rsem, lsem,
):
    rows, width = r.shape
    kv_cols = wk_hbm.shape[1]
    kv_heads = kv_cols // HEAD
    heads = wq_hbm.shape[1] // HEAD
    group = heads // kv_heads
    n_chunk, chunk = mx.shape[0], mx.shape[2] // group
    n_cp = 2 * n_x
    half = rows // 2
    cols = wr.shape[2]
    e_cols = we.shape[3]
    piece = we.shape[2]
    q_cols = wq.shape[2]
    tp, cp = lax.axis_index("tp"), lax.axis_index("cp")
    x, core = cp // 2, cp % 2

    def at_x(dx, dc=0):
        return lax.rem(x + dx + n_x, n_x) * 2 + lax.rem(core + dc, 2)

    def at_y(dy):
        return lax.rem(tp + dy + n_tp, n_tp)

    x_right, x_left, partner = {"cp": at_x(1)}, {"cp": at_x(-1)}, {"cp": at_x(0, 1)}
    y_right, y_left, y_far = {"tp": at_y(1)}, {"tp": at_y(-1)}, {"tp": at_y(2)}

    def rc(src, dst, idx, dev):
        return pltpu.make_async_remote_copy(
            src_ref=src, dst_ref=dst, send_sem=ssem.at[idx], recv_sem=rsem.at[idx], device_id=dev, device_id_type=MESH
        )

    def lc(src, dst, idx):
        return pltpu.make_async_copy(src, dst, lsem.at[idx])

    def part_of(i, size, sub=None):
        if sub is None:
            return pl.ds(pl.multiple_of(i * size, size), size)
        return pl.ds(pl.multiple_of(i * size + sub * (size // 2), size // 2), size // 2)

    halves = (slice(0, half), slice(half, rows))
    r_cols = lambda t: pl.ds(pl.multiple_of(e_cols + t * cols, HEAD), cols)
    hid_copy = lambda i: lc(hid_hbm.at[halves[i]], out.at[halves[i]], i)
    wk_copy = lambda: lc(wk_hbm, wq.at[N_Q - 2], 2)
    wv_copy = lambda: lc(wv_hbm, wq.at[N_Q - 1], 3)
    wq_copy = lambda c: lc(wq_hbm.at[:, part_of(c, q_cols)], wq.at[c], 4 + c)
    wr_copy = lambda: lc(wo_hbm.at[:, r_cols(tp)], wr.at[0], 4 + N_Q)
    kc_copy = lambda: lc(kc, kc_hbm, 5 + N_Q)
    vc_copy = lambda: lc(vc, vc_hbm, 6 + N_Q)
    we_copy = lambda j: lc(wo_hbm.at[part_of(j, piece), pl.ds(0, e_cols)], we.at[j, 0], 7 + N_Q + j)
    out_copy = lambda i: lc(out.at[part_of(i, chunk)], out_hbm.at[part_of(i, chunk)], 7 + N_Q + n_cp + i)

    top, low = pl.ds(0, half), pl.ds(half, half + POS_ROWS)

    def kv_copy(k):
        src, dst, dev = (
            ((0, top), (2, top), x_right),
            ((0, top), (3, top), x_left),
            ((0, low), (3, low), x_left),
            ((0, low), (2, low), x_right),
            ((0,), (1,), partner),
            ((2, top), (6, top), x_right),
            ((3, low), (6, low), x_left),
            ((2,), (4,), partner),
            ((3,), (5,), partner),
            ((6,), (7,), partner),
        )[k]
        return rc(kv.at[src], kv.at[dst], k, dev)

    y_devs = (y_right, y_left, y_far)
    mine = part_of(cp, piece)

    def wr_swap(k):
        return rc(wo_hbm.at[mine, r_cols(at_y((1, -1, 2)[k]))], wr.at[1 + k, mine], 10 + k, y_devs[k])

    def we_swap(k):
        return rc(wo_hbm.at[mine, pl.ds(0, e_cols)], we.at[cp, 1 + k], 13 + k, y_devs[k])

    own, right, left, far = cp, at_x(-1), at_x(1), at_x(2)
    ring = (
        (own, x_right, None), (own, x_left, None), (own, partner, None), (right, x_right, 0), (left, x_left, 1),
        (right, partner, None), (left, partner, None), (far, partner, None),
    )

    def wr_ring(m):
        src, dev, sub = ring[m]
        ref = wr.at[pl.ds(1, n_tp - 1), part_of(src, piece, sub)]
        return rc(ref, ref, 16 + m, dev)

    def we_ring(k, m):
        src, dev, sub = ring[m]
        ref = we.at[src, k] if sub is None else we.at[src, k, part_of(sub, piece // 2)]
        return rc(ref, ref, 16 + 8 * k + m, dev)

    def start_own(copy):
        for m in range(3):
            copy(m).start()

    def pass_on(copy):
        copy(0).wait_recv()
        copy(3).start()
        copy(5).start()
        copy(1).wait_recv()
        copy(4).start()
        copy(6).start()

    def pass_far(copy):
        copy(3).wait_recv()
        copy(4).wait_recv()
        copy(7).start()

    ctx_base = 16 + 8 * n_tp
    out_base = ctx_base + 4 * n_chunk

    def ctx_copy(i, k):
        src, dst, sub, dev = ((0, 1, None, y_right), (0, 2, None, y_left), (1, 3, 0, y_right), (2, 3, 1, y_left))[k]
        sl = part_of(i, chunk, sub)
        return rc(ct.at[src, sl], ct.at[dst, sl], ctx_base + 4 * i + k, dev)

    def res_copy(i, k):
        t, sub, dev = ((tp, None, y_right), (tp, None, y_left), (at_y(-1), 0, y_right), (at_y(1), 1, y_left))[k]
        ref = out.at[part_of(i, chunk, sub), r_cols(t)]
        return rc(ref, ref, out_base + 4 * i + k, dev)

    def forward(copy, i):
        copy(i, 0).wait_recv()
        copy(i, 2).start()
        copy(i, 1).wait_recv()
        copy(i, 3).start()

    barrier = pltpu.get_barrier_semaphore()
    peers = (x_right, x_left, partner) + y_devs
    for dev in peers:
        pl.semaphore_signal(barrier, inc=1, device_id=dev, device_id_type=MESH)
    hid_copy(0).start()
    wk_copy().start()
    wv_copy().start()
    hid_copy(1).start()
    for c in range(N_Q - 2):
        wq_copy(c).start()

    pos = pos_ref[...]
    pos_row = jnp.concatenate([pos[t : t + 1] for t in range(pos.shape[0])], axis=1)
    pos_q[...] = position_columns(pos_row.astype(jnp.float32))
    angles = pos_q[...] * freq_ref[...]
    lane = lax.broadcasted_iota(jnp.int32, angles.shape, 1)
    sines = jnp.sin(angles)
    cos[...] = jnp.cos(angles)
    sin[...] = jnp.where(lane < HEAD // 2, -sines, sines)
    hi = jnp.broadcast_to((pos_row // POS_BASE).astype(jnp.float32), (POS_ROWS // 2, rows))
    lo = jnp.broadcast_to(lax.rem(pos_row, POS_BASE).astype(jnp.float32), (POS_ROWS // 2, rows))
    kv[0, rows:, :] = jnp.concatenate([hi, lo], axis=0).astype(jnp.bfloat16)

    pl.semaphore_wait(barrier, len(peers))
    for k in range(n_tp - 1):
        wr_swap(k).start()
    for k in range(n_tp - 1):
        we_swap(k).start()

    for i, sl in enumerate(halves):
        hid_copy(i).wait()
        hid = out[sl, :].astype(jnp.float32)
        scaled = hid * lax.rsqrt(jnp.mean(hid * hid, axis=-1, keepdims=True) + EPS)
        r[sl, :] = (scaled * gain_ref[...]).astype(jnp.bfloat16)
        if i == 0:
            wk_copy().wait()
            wv_copy().wait()
        k = jnp.dot(r[sl, :], wq[N_Q - 2], preferred_element_type=jnp.float32)
        v = jnp.dot(r[sl, :], wq[N_Q - 1], preferred_element_type=jnp.float32).astype(jnp.bfloat16)
        kv[0, sl, kv_cols:] = v
        rots = []
        for h in range(kv_heads):
            rots.append(rope(k[:, h * HEAD : (h + 1) * HEAD], cos[sl, :], sin[sl, :]))
            kv[0, sl, h * HEAD : (h + 1) * HEAD] = rots[h]
        if i == 0:
            kv_copy(0).start()
            kv_copy(1).start()
        else:
            kv_copy(2).start()
            kv_copy(3).start()
            kv_copy(4).start()
        kc[sl] = jnp.stack(rots, axis=1)
        vc[sl] = jnp.stack([v[:, h * HEAD : (h + 1) * HEAD] for h in range(kv_heads)], axis=1)
    for c in range(N_Q - 2, N_Q):
        wq_copy(c).start()
    kc_copy().start()
    vc_copy().start()
    wr_copy().start()
    for j in range(n_cp):
        we_copy(j).start()

    @pl.loop(0, N_Q)
    def _(c):
        wq_copy(c).wait()
        qc = jnp.dot(r[...], wq[c], preferred_element_type=jnp.float32)
        per = q_cols // HEAD
        for j in range(per):
            rot = rope(qc[:, j * HEAD : (j + 1) * HEAD], cos[...], sin[...])
            head = c * per + j
            kvh, g = head // group, lax.rem(head, group)
            for i in range(n_chunk):
                q[i, kvh, part_of(g, chunk), :] = rot[i * chunk : (i + 1) * chunk]

    mx[...] = jnp.full_like(mx, NEG_BIG)
    ls[...] = jnp.zeros_like(ls)
    acc[...] = jnp.zeros_like(acc)
    scale = HEAD**-0.5 * LOG2E

    def attend(i, slot):
        hi = kv[slot, pl.ds(rows, POS_ROWS // 2), :].astype(jnp.float32)
        lo = kv[slot, pl.ds(rows + POS_ROWS // 2, POS_ROWS // 2), :].astype(jnp.float32)
        pos_k = (hi * POS_BASE + lo)[0:1, :]
        pos_i = pos_q[part_of(i, chunk), :]
        n_l = rows // HEAD
        bias = jnp.concatenate(
            [jnp.where(pos_k[:, t * HEAD : (t + 1) * HEAD] <= pos_i, 0.0, NEG_BIG) for t in range(n_l)], axis=1
        )
        for kvh in range(kv_heads):
            k_blk = kv[slot, pl.ds(0, rows), kvh * HEAD : (kvh + 1) * HEAD]
            v_blk = kv[slot, pl.ds(0, rows), kv_cols + kvh * HEAD : kv_cols + (kvh + 1) * HEAD]
            s = lax.dot_general(q[i, kvh], k_blk, (((1,), (1,)), ((), ())), preferred_element_type=jnp.float32)
            s = (s.reshape(group, chunk, rows) * scale + bias[None]).reshape(group * chunk, rows)
            m_old = mx[i, kvh]
            m_new = jnp.maximum(m_old, jnp.max(s, axis=1, keepdims=True))
            alpha = jnp.exp2(m_old - m_new)
            p = jnp.exp2(s - jnp.concatenate([m_new] * n_l, axis=1))
            part = p[:, :HEAD]
            for t in range(1, n_l):
                part = part + p[:, t * HEAD : (t + 1) * HEAD]
            mx[i, kvh] = m_new
            ls[i, kvh] = ls[i, kvh] * alpha + part
            acc[i, kvh] = acc[i, kvh] * alpha + jnp.dot(
                p.astype(jnp.bfloat16), v_blk, preferred_element_type=jnp.float32
            )

    n_lead = n_chunk // 2

    def attend_pair(first):
        @pl.loop(0, 2 * n_lead)
        def _(t):
            attend(t // 2, first + lax.rem(t, 2))

    def finish(i):
        for kvh in range(kv_heads):
            total = jnp.sum(ls[i, kvh], axis=1, keepdims=True)
            ctx = (acc[i, kvh] / total).astype(jnp.bfloat16)
            for g in range(group):
                h = kvh * group + g
                ct[0, part_of(i, chunk), h * HEAD : (h + 1) * HEAD] = ctx[g * chunk : (g + 1) * chunk]
        ctx_copy(i, 0).start()
        ctx_copy(i, 1).start()

    kv_copy(0).wait_recv()
    kv_copy(5).start()
    kv_copy(2).wait_recv()
    kv_copy(6).start()
    kv_copy(4).wait_recv()
    attend_pair(0)
    for k in range(n_tp - 1):
        wr_swap(k).wait_recv()
    kv_copy(1).wait_recv()
    kv_copy(3).wait_recv()
    kv_copy(7).start()
    kv_copy(8).start()
    start_own(wr_ring)
    attend_pair(2)
    kv_copy(5).wait_recv()
    kv_copy(6).wait_recv()
    kv_copy(9).start()
    kv_copy(7).wait_recv()
    kv_copy(8).wait_recv()
    attend_pair(4)
    kv_copy(9).wait_recv()

    @pl.loop(0, n_lead)
    def _(i):
        attend(i, 6)
        attend(i, 7)
        finish(i)

    we_k = lambda k: functools.partial(we_ring, k)
    for k in range(n_tp - 1):
        we_swap(k).wait_recv()
    start_own(we_k(1))

    def late_chunk(i):
        @pl.loop(0, n_cp)
        def _(slot):
            attend(i, slot)

        finish(i)
        forward(ctx_copy, i - n_lead)

    late_chunk(n_lead)
    pass_on(wr_ring)
    for k in range(2, n_tp):
        start_own(we_k(k))
    late_chunk(n_lead + 1)
    pass_on(we_k(1))
    forward(ctx_copy, n_lead)
    pass_far(wr_ring)
    pass_on(we_k(2))
    forward(ctx_copy, n_lead + 1)
    for m in (2, 5, 6, 7):
        wr_ring(m).wait_recv()
    wr_copy().wait()

    @pl.loop(0, n_chunk)
    def _(i):
        ctx_copy(i, 2).wait_recv()
        ctx_copy(i, 3).wait_recv()
        sl = part_of(i, chunk)
        proj = jnp.dot(ct[0, sl, :], wr[0], preferred_element_type=jnp.float32)
        for t in range(1, n_tp):
            proj = proj + jnp.dot(ct[t, sl, :], wr[t], preferred_element_type=jnp.float32)
        out[sl, r_cols(tp)] = (out[sl, r_cols(tp)].astype(jnp.float32) + proj).astype(jnp.bfloat16)
        res_copy(i, 0).start()
        res_copy(i, 1).start()

    e_tile = 512
    n_e = e_cols // e_tile

    def project(j, first=False, last=False):
        ctx = jnp.concatenate([ct[t, :, part_of(j, piece)] for t in range(n_tp)], axis=1)

        @pl.loop(0, n_e)
        def _(n):
            sl = part_of(n, e_tile)
            w = we[j, :, :, sl].reshape(n_tp * piece, e_tile)
            add = jnp.dot(ctx, w, preferred_element_type=jnp.float32)
            if not first:
                add = acc_e[:, sl] + add
            if last:
                out[:, sl] = (out[:, sl].astype(jnp.float32) + add).astype(jnp.bfloat16)
            else:
                acc_e[:, sl] = add

    for j in range(n_cp):
        we_copy(j).wait()
    pass_on(we_k(3))
    project(own, first=True)
    forward(res_copy, 0)
    for k in range(1, n_tp):
        we_k(k)(2).wait_recv()
    project(at_x(0, 1))
    project(right)
    forward(res_copy, 1)
    project(left)
    forward(res_copy, 2)
    for k in range(1, n_tp):
        we_k(k)(5).wait_recv()
    project(at_x(-1, 1))
    for k in range(1, n_tp):
        we_k(k)(6).wait_recv()
    forward(res_copy, 3)
    project(at_x(1, 1))
    for k in range(1, n_tp):
        pass_far(we_k(k))
    project(far)
    for k in range(1, n_tp):
        we_k(k)(7).wait_recv()
    project(at_x(2, 1), last=True)

    @pl.loop(0, n_chunk)
    def _(i):
        res_copy(i, 2).wait_recv()
        res_copy(i, 3).wait_recv()
        out_copy(i).start()

    kc_copy().wait()
    vc_copy().wait()
    for k in range(10):
        kv_copy(k).wait_send()
    for k in range(n_tp - 1):
        wr_swap(k).wait_send()
        we_swap(k).wait_send()
    for m in range(8):
        wr_ring(m).wait_send()
        for k in range(1, n_tp):
            we_ring(k, m).wait_send()

    @pl.loop(0, n_chunk)
    def _(i):
        for k in range(4):
            ctx_copy(i, k).wait_send()
            res_copy(i, k).wait_send()
        out_copy(i).wait()


def attention_block(mesh, pos, freq, gain, hidden, w_key, w_value, w_query, w_out):
    n_tp, n_cp = mesh.shape["tp"], mesh.shape["cp"]
    rows, width = hidden.shape
    kv_cols = w_key.shape[1]
    heads, kv_heads = w_query.shape[1] // HEAD, kv_cols // HEAD
    n_chunk = 4
    grp = heads // kv_heads * (rows // n_chunk)
    e_cols = width * E_FRACTION[0] // E_FRACTION[1]
    cols = (width - e_cols) // n_tp
    k_rows = w_out.shape[0]
    bf16, f32 = jnp.bfloat16, jnp.float32
    n_sem = 16 + 8 * n_tp + 8 * n_chunk
    cache = (rows, kv_heads, HEAD)
    return pl.pallas_call(
        functools.partial(block_kernel, n_tp, n_cp // 2),
        out_shape=[jax.ShapeDtypeStruct(s, bf16) for s in ((rows, width), cache, cache)],
        in_specs=[vmem_spec()] * 3 + [any_spec()] * 5,
        out_specs=[any_spec()] * 3,
        scratch_shapes=[
            pltpu.VMEM((n_cp, rows + POS_ROWS, 2 * kv_cols), bf16),
            pltpu.VMEM((rows, width), bf16),
            pltpu.VMEM((rows, HEAD), f32),
            pltpu.VMEM((rows, HEAD), f32),
            pltpu.VMEM((N_Q, width, w_query.shape[1] // N_Q), bf16),
            pltpu.VMEM((n_tp, k_rows, cols), bf16),
            pltpu.VMEM((n_cp, n_tp, k_rows // n_cp, e_cols), bf16),
            pltpu.VMEM((n_tp, rows, k_rows), bf16),
            pltpu.VMEM((n_chunk, kv_heads, grp, HEAD), bf16),
            pltpu.VMEM((n_chunk, kv_heads, grp, HEAD), f32),
            pltpu.VMEM((n_chunk, kv_heads, grp, HEAD), f32),
            pltpu.VMEM((n_chunk, kv_heads, grp, HEAD), f32),
            pltpu.VMEM((rows, e_cols), f32),
            pltpu.VMEM((rows, HEAD), f32),
            pltpu.VMEM((rows, width), bf16),
            pltpu.VMEM(cache, bf16),
            pltpu.VMEM(cache, bf16),
            pltpu.SemaphoreType.DMA((n_sem,)),
            pltpu.SemaphoreType.DMA((n_sem,)),
            pltpu.SemaphoreType.DMA((32,)),
        ],
        compiler_params=pltpu.CompilerParams(collective_id=0, has_side_effects=True, vmem_limit_bytes=VMEM_LIMIT),
        name="attention_block",
    )(pos, freq, gain, hidden, w_key, w_value, w_query, w_out)


def copy_kernel(src, k_src, v_src, dst, k_dst, v_dst, buf, k_buf, v_buf, isem, osem):
    n = buf.shape[0]
    tile = src.shape[0] // n
    rows = lambda i: pl.ds(i * tile, tile)
    moves = [(src.at[rows(i)], buf.at[i], dst.at[rows(i)]) for i in range(n)]
    moves += [(k_src, k_buf, k_dst), (v_src, v_buf, v_dst)]
    for i, (a, b, _) in enumerate(moves):
        pltpu.make_async_copy(a, b, isem.at[i]).start()
    for i, (a, b, c) in enumerate(moves):
        pltpu.make_async_copy(a, b, isem.at[i]).wait()
        pltpu.make_async_copy(b, c, osem.at[i]).start()
    for i, (_, b, c) in enumerate(moves):
        pltpu.make_async_copy(b, c, osem.at[i]).wait()


def copy_out(*arrs):
    n = 8
    rows, width = arrs[0].shape
    return pl.pallas_call(
        copy_kernel,
        in_specs=[any_spec()] * 3,
        out_specs=[any_spec()] * 3,
        out_shape=[jax.ShapeDtypeStruct(a.shape, a.dtype) for a in arrs],
        scratch_shapes=[
            pltpu.VMEM((n, rows // n, width), arrs[0].dtype),
            *(pltpu.VMEM(a.shape, a.dtype) for a in arrs[1:]),
            pltpu.SemaphoreType.DMA((n + 2,)),
            pltpu.SemaphoreType.DMA((n + 2,)),
        ],
        name="copy_out",
    )(*arrs)


def solution(mesh):
    def local_block(hidden, tok_pos, norm_gain, w_query, w_key, w_value, w_out):
        results = attention_block(
            mesh, tok_pos.reshape(-1, HEAD), inv_freq_row(), norm_gain[None, :], hidden, w_key, w_value, w_query, w_out
        )
        return tuple(copy_out(*results))

    row_spec = P(("dp", "cp"), None)
    cache_spec = P(("dp", "cp"), "tp", None)
    return jax.shard_map(
        local_block,
        mesh=mesh,
        in_specs=(row_spec, P(("dp", "cp")), P(None), P(None, "tp"), P(None, "tp"), P(None, "tp"), P("tp", None)),
        out_specs=(row_spec, cache_spec, cache_spec),
        check_vma=False,
    )
```

time: 333 us -> 103 us (0.31)
  waiting for transfers between devices: 179 us -> 0 us
  Pallas kernels: 0 us -> 102 us
  matrix products: 66.6 us -> 0 us
  other arithmetic: 31.2 us -> 0.6 us
  starting transfers between devices: 24.4 us -> 0 us
  local copies, waits for them, and re-layouts: 16.4 us -> 0 us
  between operations: 14.3 us -> 0.8 us
    psum x1 -> x0, waiting for transfers between devices: 158 us -> none  [local_block(): attn_proj = lax.psum(part_proj, 'tp')]
    pallas_call x0 -> x2, Pallas kernels: none -> 102 us  [the longest x1 97.7 us: attention_block(): pl.pallas_call(functools.partial(block_kernel, n_tp, n_cp // 2), out_shap...]
    dot_general x20 -> x0, matrix products: 66.6 us -> none  [the longest x8 26.3 us: absorb(): jnp.einsum('kgqt,tkd->kgqd', exp_scores.astype(jnp.bfloat16), v_blk, pref...]
    ppermute x21 -> x0, starting transfers between devices: 24.3 us -> none  [the longest x7 12.6 us: step(): k_blk = lax.ppermute(k_blk, 'cp', shift_pairs)]
    ppermute x21 -> x0, waiting for transfers between devices: 21 us -> none  [the longest x7 21 us: step(): pos_blk = lax.ppermute(pos_blk, 'cp', shift_pairs)]
    reduce_sum x9 -> x0, other arithmetic: 17.3 us -> none  [the longest x8 14.2 us: absorb(): row_sum = row_sum * rescale + jnp.sum(exp_scores, axis=-1)]
    while x57 -> x0, local copies, waits for them, and re-layouts: 10.4 us -> none
    convert_element_type x2 -> x0, other arithmetic: 8.69 us -> none  [the longest x1 8 us: local_block(): hidden_out = (hid_f32 + attn_proj).astype(jnp.bfloat16)]
  transfers between devices with their start and end apart: 22 -> 0, of which waited for: 8 -> 0; matrix products, arithmetic and copies ran while one was open for 8% -> 0% of each run, Pallas kernels for 0% -> 0%
where the time goes in v3:
time: 103 us
  Pallas kernels  102 us (99%)
    pallas_call x1, Pallas kernels, attention_block(): pl.pallas_call(functools.partial(block_kernel, n_tp, n_cp // 2), out_shap...  97.7 us
    pallas_call x1, Pallas kernels, copy_out(): pl.pallas_call(copy_kernel, in_specs=[any_spec()] * 3, out_specs=[any_spe...  4.07 us

profile of v3, /device:TPU:97, one launch (start us, length us, event | category | flops | bytes accessed | tf_op | source)
XLA Modules:
  0.0 103.2 jit_solution(3767311509645832789)
XLA Ops:
  0.6 0.6 maximum_bitcast_fusion.freq_ref
  1.2 97.7 %attention_block.1 = (bf16[512,4096]{1,0:T(8,128)(2,1)}, bf16[512,2,128]{2,1,0:T(2,128)(2,1)}, bf16[512,2,128]{2,1,0:T(2,128)(2,1)}) custom-call(s32[4,128]{1,0:T(4,128)} %bitcast.5, f32[1,128]{1,0:T(1,128)} %maximum_bitcast_fusion.freq_ref, f32[1,4096]{1,0:T(1,128)} %bitcast.4, bf16[512,4096]{1,0:T(8,128)(2,1)} %hid_hbm.1, bf16[4096,256]{1,0:T(8,128)(2,1)} %wk_hbm.1, ...), custom_call_target="tpu_custom_call" | custom-call | tf_op jit(solution)/shard_map/attention_block/pallas_call | solution.py:452
  99.0 4.1 %copy_out.1 = (bf16[512,4096]{1,0:T(8,128)(2,1)}, bf16[512,2,128]{2,1,0:T(2,128)(2,1)}, bf16[512,2,128]{2,1,0:T(2,128)(2,1)}) custom-call(bf16[512,4096]{1,0:T(8,128)(2,1)} %get-tuple-element.6.src, bf16[512,2,128]{2,1,0:T(2,128)(2,1)} %get-tuple-element.7.k_src, bf16[512,2,128]{2,1,0:T(2,128)(2,1)} %get-tuple-element.8.v_src), custom_call_target="tpu_custom_call" | custom-call | tf_op jit(solution)/shard_map/copy_out/pallas_call | solution.py:502
  (1 shorter events, 0.0 us)

commit v4 on v3

--- a/solution.py
+++ b/solution.py
@@ -2,6 +2,7 @@
 
 import jax
 import jax.numpy as jnp
+import numpy as np
 from jax import lax
 from jax.experimental import pallas as pl
 from jax.experimental.pallas import tpu as pltpu
@@ -29,8 +30,8 @@
 
 
 def inv_freq_row():
-    freq = 1.0 / (THETA ** (jnp.arange(0, HEAD, 2, dtype=jnp.float32) / HEAD))
-    return jnp.concatenate([freq, freq])[None, :]
+    freq = 1.0 / (np.float64(THETA) ** (np.arange(0, HEAD, 2) / HEAD))
+    return jnp.asarray(np.concatenate([freq, freq])[None, :], jnp.float32)
 
 
 def rope(head_f32, cos_full, sin_full):
@@ -47,8 +48,8 @@
 
 
 def block_kernel(
-    n_tp, n_x, pos_ref, freq_ref, gain_ref, hid_hbm, wk_hbm, wv_hbm, wq_hbm, wo_hbm, out_hbm, kc_hbm, vc_hbm,
-    kv, r, cos, sin, wq, wr, we, ct, q, mx, ls, acc, acc_e, pos_q, out, kc, vc, ssem, rsem, lsem,
+    n_tp, n_x, pos_ref, freq_ref, gain_ref, hid_hbm, wk_hbm, wv_hbm, wq_hbm, wo_hbm, out, kc, vc,
+    kv, r, cos, sin, wq, wr, we, ct, q, mx, ls, acc, acc_e, pos_q, ssem, rsem, lsem,
 ):
     rows, width = r.shape
     kv_cols = wk_hbm.shape[1]
@@ -57,6 +58,7 @@
     group = heads // kv_heads
     n_chunk, chunk = mx.shape[0], mx.shape[2] // group
     n_cp = 2 * n_x
+    n_ring = 18 + 8 * n_tp
     half = rows // 2
     cols = wr.shape[2]
     e_cols = we.shape[3]
@@ -87,24 +89,23 @@
             return pl.ds(pl.multiple_of(i * size, size), size)
         return pl.ds(pl.multiple_of(i * size + sub * (size // 2), size // 2), size // 2)
 
-    halves = (slice(0, half), slice(half, rows))
+    quarter = half // 2
+    parts = (slice(0, quarter), slice(quarter, half), slice(half, rows))
     r_cols = lambda t: pl.ds(pl.multiple_of(e_cols + t * cols, HEAD), cols)
-    hid_copy = lambda i: lc(hid_hbm.at[halves[i]], out.at[halves[i]], i)
-    wk_copy = lambda: lc(wk_hbm, wq.at[N_Q - 2], 2)
-    wv_copy = lambda: lc(wv_hbm, wq.at[N_Q - 1], 3)
-    wq_copy = lambda c: lc(wq_hbm.at[:, part_of(c, q_cols)], wq.at[c], 4 + c)
-    wr_copy = lambda: lc(wo_hbm.at[:, r_cols(tp)], wr.at[0], 4 + N_Q)
-    kc_copy = lambda: lc(kc, kc_hbm, 5 + N_Q)
-    vc_copy = lambda: lc(vc, vc_hbm, 6 + N_Q)
-    we_copy = lambda j: lc(wo_hbm.at[part_of(j, piece), pl.ds(0, e_cols)], we.at[j, 0], 7 + N_Q + j)
-    out_copy = lambda i: lc(out.at[part_of(i, chunk)], out_hbm.at[part_of(i, chunk)], 7 + N_Q + n_cp + i)
+    hid_copy = lambda i: lc(hid_hbm.at[parts[i]], out.at[parts[i]], i)
+    wk_copy = lambda: lc(wk_hbm, wq.at[N_Q - 2], 3)
+    wv_copy = lambda: lc(wv_hbm, wq.at[N_Q - 1], 4)
+    wq_copy = lambda c: lc(wq_hbm.at[:, part_of(c, q_cols)], wq.at[c], 5 + c)
+    wr_copy = lambda: lc(wo_hbm.at[:, r_cols(tp)], wr.at[0], 5 + N_Q)
+    we_copy = lambda j: lc(wo_hbm.at[part_of(j, piece), pl.ds(0, e_cols)], we.at[j, 0], 6 + N_Q + j)
 
     top, low = pl.ds(0, half), pl.ds(half, half + POS_ROWS)
+    top_a, top_b = pl.ds(0, quarter), pl.ds(quarter, quarter)
 
     def kv_copy(k):
         src, dst, dev = (
-            ((0, top), (2, top), x_right),
-            ((0, top), (3, top), x_left),
+            ((0, top_a), (2, top_a), x_right),
+            ((0, top_a), (3, top_a), x_left),
             ((0, low), (3, low), x_left),
             ((0, low), (2, low), x_right),
             ((0,), (1,), partner),
@@ -113,8 +114,10 @@
             ((2,), (4,), partner),
             ((3,), (5,), partner),
             ((6,), (7,), partner),
+            ((0, top_b), (2, top_b), x_right),
+            ((0, top_b), (3, top_b), x_left),
         )[k]
-        return rc(kv.at[src], kv.at[dst], k, dev)
+        return rc(kv.at[src], kv.at[dst], k if k < 10 else n_ring - 2 + k - 10, dev)
 
     y_devs = (y_right, y_left, y_far)
     mine = part_of(cp, piece)
@@ -158,7 +161,7 @@
         copy(4).wait_recv()
         copy(7).start()
 
-    ctx_base = 16 + 8 * n_tp
+    ctx_base = n_ring
     out_base = ctx_base + 4 * n_chunk
 
     def ctx_copy(i, k):
@@ -185,6 +188,7 @@
     wk_copy().start()
     wv_copy().start()
     hid_copy(1).start()
+    hid_copy(2).start()
     for c in range(N_Q - 2):
         wq_copy(c).start()
 
@@ -200,13 +204,7 @@
     lo = jnp.broadcast_to(lax.rem(pos_row, POS_BASE).astype(jnp.float32), (POS_ROWS // 2, rows))
     kv[0, rows:, :] = jnp.concatenate([hi, lo], axis=0).astype(jnp.bfloat16)
 
-    pl.semaphore_wait(barrier, len(peers))
-    for k in range(n_tp - 1):
-        wr_swap(k).start()
-    for k in range(n_tp - 1):
-        we_swap(k).start()
-
-    for i, sl in enumerate(halves):
+    for i, sl in enumerate(parts):
         hid_copy(i).wait()
         hid = out[sl, :].astype(jnp.float32)
         scaled = hid * lax.rsqrt(jnp.mean(hid * hid, axis=-1, keepdims=True) + EPS)
@@ -222,8 +220,16 @@
             rots.append(rope(k[:, h * HEAD : (h + 1) * HEAD], cos[sl, :], sin[sl, :]))
             kv[0, sl, h * HEAD : (h + 1) * HEAD] = rots[h]
         if i == 0:
+            pl.semaphore_wait(barrier, len(peers))
             kv_copy(0).start()
             kv_copy(1).start()
+            for t in range(n_tp - 1):
+                wr_swap(t).start()
+            for t in range(n_tp - 1):
+                we_swap(t).start()
+        elif i == 1:
+            kv_copy(10).start()
+            kv_copy(11).start()
         else:
             kv_copy(2).start()
             kv_copy(3).start()
@@ -232,8 +238,6 @@
         vc[sl] = jnp.stack([v[:, h * HEAD : (h + 1) * HEAD] for h in range(kv_heads)], axis=1)
     for c in range(N_Q - 2, N_Q):
         wq_copy(c).start()
-    kc_copy().start()
-    vc_copy().start()
     wr_copy().start()
     for j in range(n_cp):
         we_copy(j).start()
@@ -284,10 +288,10 @@
 
     n_lead = n_chunk // 2
 
-    def attend_pair(first):
-        @pl.loop(0, 2 * n_lead)
+    def attend_all(chunks, first, n_slot):
+        @pl.loop(0, (chunks[1] - chunks[0]) * n_slot)
         def _(t):
-            attend(t // 2, first + lax.rem(t, 2))
+            attend(chunks[0] + t // n_slot, first + lax.rem(t, n_slot))
 
     def finish(i):
         for kvh in range(kv_heads):
@@ -299,32 +303,44 @@
         ctx_copy(i, 0).start()
         ctx_copy(i, 1).start()
 
+    attend_all((0, 1), 0, 1)
     kv_copy(0).wait_recv()
+    kv_copy(10).wait_recv()
     kv_copy(5).start()
+    attend_all((1, n_lead), 0, 1)
+    kv_copy(4).wait_recv()
+    attend_all((0, n_lead), 1, 1)
     kv_copy(2).wait_recv()
     kv_copy(6).start()
-    kv_copy(4).wait_recv()
-    attend_pair(0)
-    for k in range(n_tp - 1):
-        wr_swap(k).wait_recv()
+    attend_all((n_lead, n_lead + 1), 0, 2)
+    for t in range(n_tp - 1):
+        wr_swap(t).wait_recv()
     kv_copy(1).wait_recv()
+    kv_copy(11).wait_recv()
     kv_copy(3).wait_recv()
     kv_copy(7).start()
     kv_copy(8).start()
     start_own(wr_ring)
-    attend_pair(2)
+    attend_all((0, 1), 2, 2)
+    kv_copy(7).wait_recv()
+    kv_copy(8).wait_recv()
+    attend_all((0, 1), 4, 2)
+    attend_all((1, n_lead), 2, 1)
     kv_copy(5).wait_recv()
     kv_copy(6).wait_recv()
     kv_copy(9).start()
-    kv_copy(7).wait_recv()
-    kv_copy(8).wait_recv()
-    attend_pair(4)
+    attend_all((0, 1), 6, 1)
+    attend_all((1, n_lead), 3, 1)
     kv_copy(9).wait_recv()
-
-    @pl.loop(0, n_lead)
+    attend_all((0, 1), 7, 1)
+    finish(0)
+
+    @pl.loop(1, n_lead)
     def _(i):
-        attend(i, 6)
-        attend(i, 7)
+        @pl.loop(4, n_cp)
+        def _(slot):
+            attend(i, slot)
+
         finish(i)
 
     we_k = lambda k: functools.partial(we_ring, k)
@@ -332,19 +348,19 @@
         we_swap(k).wait_recv()
     start_own(we_k(1))
 
-    def late_chunk(i):
-        @pl.loop(0, n_cp)
+    def late_chunk(i, first):
+        @pl.loop(first, n_cp)
         def _(slot):
             attend(i, slot)
 
         finish(i)
         forward(ctx_copy, i - n_lead)
 
-    late_chunk(n_lead)
+    late_chunk(n_lead, 2)
     pass_on(wr_ring)
     for k in range(2, n_tp):
         start_own(we_k(k))
-    late_chunk(n_lead + 1)
+    late_chunk(n_lead + 1, 0)
     pass_on(we_k(1))
     forward(ctx_copy, n_lead)
     pass_far(wr_ring)
@@ -394,17 +410,18 @@
     project(at_x(0, 1))
     project(right)
     forward(res_copy, 1)
+    pass_far(we_k(1))
     project(left)
     forward(res_copy, 2)
+    pass_far(we_k(2))
     for k in range(1, n_tp):
         we_k(k)(5).wait_recv()
     project(at_x(-1, 1))
     for k in range(1, n_tp):
         we_k(k)(6).wait_recv()
     forward(res_copy, 3)
+    pass_far(we_k(3))
     project(at_x(1, 1))
-    for k in range(1, n_tp):
-        pass_far(we_k(k))
     project(far)
     for k in range(1, n_tp):
         we_k(k)(7).wait_recv()
@@ -414,11 +431,8 @@
     def _(i):
         res_copy(i, 2).wait_recv()
         res_copy(i, 3).wait_recv()
-        out_copy(i).start()
-
-    kc_copy().wait()
-    vc_copy().wait()
-    for k in range(10):
+
+    for k in range(12):
         kv_copy(k).wait_send()
     for k in range(n_tp - 1):
         wr_swap(k).wait_send()
@@ -433,7 +447,6 @@
         for k in range(4):
             ctx_copy(i, k).wait_send()
             res_copy(i, k).wait_send()
-        out_copy(i).wait()
 
 
 def attention_block(mesh, pos, freq, gain, hidden, w_key, w_value, w_query, w_out):
@@ -447,13 +460,13 @@
     cols = (width - e_cols) // n_tp
     k_rows = w_out.shape[0]
     bf16, f32 = jnp.bfloat16, jnp.float32
-    n_sem = 16 + 8 * n_tp + 8 * n_chunk
+    n_sem = 18 + 8 * n_tp + 8 * n_chunk
     cache = (rows, kv_heads, HEAD)
     return pl.pallas_call(
         functools.partial(block_kernel, n_tp, n_cp // 2),
-        out_shape=[jax.ShapeDtypeStruct(s, bf16) for s in ((rows, width), cache, cache)],
+        out_shape=[pltpu.VMEM(s, bf16) for s in ((rows, width), cache, cache)],
         in_specs=[vmem_spec()] * 3 + [any_spec()] * 5,
-        out_specs=[any_spec()] * 3,
+        out_specs=[vmem_spec()] * 3,
         scratch_shapes=[
             pltpu.VMEM((n_cp, rows + POS_ROWS, 2 * kv_cols), bf16),
             pltpu.VMEM((rows, width), bf16),
@@ -469,47 +482,37 @@
             pltpu.VMEM((n_chunk, kv_heads, grp, HEAD), f32),
             pltpu.VMEM((rows, e_cols), f32),
             pltpu.VMEM((rows, HEAD), f32),
-            pltpu.VMEM((rows, width), bf16),
-            pltpu.VMEM(cache, bf16),
-            pltpu.VMEM(cache, bf16),
             pltpu.SemaphoreType.DMA((n_sem,)),
             pltpu.SemaphoreType.DMA((n_sem,)),
-            pltpu.SemaphoreType.DMA((32,)),
+            pltpu.SemaphoreType.DMA((6 + N_Q + n_cp,)),
         ],
-        compiler_params=pltpu.CompilerParams(collective_id=0, has_side_effects=True, vmem_limit_bytes=VMEM_LIMIT),
+        compiler_params=pltpu.CompilerParams(collective_id=0, has_side_effects=True, vmem_limit_bytes=VMEM_LIMIT - 5 * 2**20),
         name="attention_block",
     )(pos, freq, gain, hidden, w_key, w_value, w_query, w_out)
 
 
-def copy_kernel(src, k_src, v_src, dst, k_dst, v_dst, buf, k_buf, v_buf, isem, osem):
-    n = buf.shape[0]
+def copy_kernel(src, k_src, v_src, dst, k_dst, v_dst, sem):
+    n = 4
     tile = src.shape[0] // n
     rows = lambda i: pl.ds(i * tile, tile)
-    moves = [(src.at[rows(i)], buf.at[i], dst.at[rows(i)]) for i in range(n)]
-    moves += [(k_src, k_buf, k_dst), (v_src, v_buf, v_dst)]
-    for i, (a, b, _) in enumerate(moves):
-        pltpu.make_async_copy(a, b, isem.at[i]).start()
-    for i, (a, b, c) in enumerate(moves):
-        pltpu.make_async_copy(a, b, isem.at[i]).wait()
-        pltpu.make_async_copy(b, c, osem.at[i]).start()
-    for i, (_, b, c) in enumerate(moves):
-        pltpu.make_async_copy(b, c, osem.at[i]).wait()
+    copies = [pltpu.make_async_copy(src.at[rows(i)], dst.at[rows(i)], sem.at[i]) for i in range(n)]
+    copies.append(pltpu.make_async_copy(k_src, k_dst, sem.at[n]))
+    copies.append(pltpu.make_async_copy(v_src, v_dst, sem.at[n + 1]))
+    for cpy in copies:
+        cpy.start()
+    for cpy in copies:
+        cpy.wait()
 
 
 def copy_out(*arrs):
-    n = 8
-    rows, width = arrs[0].shape
+    arrs = [pltpu.with_memory_space_constraint(a, pltpu.VMEM) for a in arrs]
     return pl.pallas_call(
         copy_kernel,
-        in_specs=[any_spec()] * 3,
+        in_specs=[vmem_spec()] * 3,
         out_specs=[any_spec()] * 3,
         out_shape=[jax.ShapeDtypeStruct(a.shape, a.dtype) for a in arrs],
-        scratch_shapes=[
-            pltpu.VMEM((n, rows // n, width), arrs[0].dtype),
-            *(pltpu.VMEM(a.shape, a.dtype) for a in arrs[1:]),
-            pltpu.SemaphoreType.DMA((n + 2,)),
-            pltpu.SemaphoreType.DMA((n + 2,)),
-        ],
+        scratch_shapes=[pltpu.SemaphoreType.DMA((8,))],
+        compiler_params=pltpu.CompilerParams(vmem_limit_bytes=4 * 2**20),
         name="copy_out",
     )(*arrs)
 

time: 103 us -> 96.1 us (0.933)
  Pallas kernels: 102 us -> 95.2 us
    pallas_call x1, Pallas kernels: 97.7 us -> 92.9 us  [attention_block(): pl.pallas_call(functools.partial(block_kernel, n_tp, n_cp // 2), out_shap...]
    pallas_call x1, Pallas kernels: 4.07 us -> 2.24 us  [copy_out(): pl.pallas_call(copy_kernel, in_specs=[vmem_spec()] * 3, out_specs=[any_sp...]
where the time goes in v4:
time: 96.1 us; the launch traced here: 96 us
  Pallas kernels  95.2 us (99%)
    pallas_call x1, Pallas kernels, attention_block(): pl.pallas_call(functools.partial(block_kernel, n_tp, n_cp // 2), out_shap...  92.9 us
    pallas_call x1, Pallas kernels, copy_out(): pl.pallas_call(copy_kernel, in_specs=[vmem_spec()] * 3, out_specs=[any_sp...  2.24 us

profile of v4, /device:TPU:97, one launch (start us, length us, event | category | flops | bytes accessed | tf_op | source)
XLA Modules:
  0.0 96.0 jit_solution(16949802558499226371)
XLA Ops:
  0.6 92.9 %attention_block.1 = (bf16[512,4096]{1,0:T(8,128)(2,1)S(1)}, bf16[512,2,128]{2,1,0:T(2,128)(2,1)S(1)}, bf16[512,2,128]{2,1,0:T(2,128)(2,1)S(1)}) custom-call(s32[4,128]{1,0:T(4,128)} %bitcast.3, f32[1,128]{1,0:T(1,128)} %constant.2.clone.freq_ref, f32[1,4096]{1,0:T(1,128)} %bitcast.2, bf16[512,4096]{1,0:T(8,128)(2,1)} %hid_hbm.1, bf16[4096,256]{1,0:T(8,128)(2,1)} %wk_hbm.1, ...), custom_call_target="tpu_custom_call" | custom-call | tf_op jit(solution)/shard_map/attention_block/pallas_call | solution.py:465
  93.6 2.2 %copy_out.1 = (bf16[512,4096]{1,0:T(8,128)(2,1)}, bf16[512,2,128]{2,1,0:T(2,128)(2,1)}, bf16[512,2,128]{2,1,0:T(2,128)(2,1)}) custom-call(bf16[512,4096]{1,0:T(8,128)(2,1)S(1)} %get-tuple-element.6.src, bf16[512,2,128]{2,1,0:T(2,128)(2,1)S(1)} %get-tuple-element.7.k_src, bf16[512,2,128]{2,1,0:T(2,128)(2,1)S(1)} %get-tuple-element.8.v_src), custom_call_target="tpu_custom_call" | custom-call | tf_op jit(solution)/shard_map/copy_out/pallas_call | solution.py:509

commit v5 on v4

--- a/solution.py
+++ b/solution.py
@@ -48,8 +48,8 @@
 
 
 def block_kernel(
-    n_tp, n_x, pos_ref, freq_ref, gain_ref, hid_hbm, wk_hbm, wv_hbm, wq_hbm, wo_hbm, out, kc, vc,
-    kv, r, cos, sin, wq, wr, we, ct, q, mx, ls, acc, acc_e, pos_q, ssem, rsem, lsem,
+    n_tp, n_x, pos_hbm, freq_hbm, gain_hbm, hid_hbm, wk_hbm, wv_hbm, wq_hbm, wo_hbm, out, kc, vc,
+    kv, r, cos, sin, wq, wr, we, ct, q, mx, ls, acc, acc_e, pos_q, pos_ref, freq_ref, gain_ref, ssem, rsem, lsem,
 ):
     rows, width = r.shape
     kv_cols = wk_hbm.shape[1]
@@ -58,7 +58,7 @@
     group = heads // kv_heads
     n_chunk, chunk = mx.shape[0], mx.shape[2] // group
     n_cp = 2 * n_x
-    n_ring = 18 + 8 * n_tp
+    n_ring = 24 + 8 * n_tp
     half = rows // 2
     cols = wr.shape[2]
     e_cols = we.shape[3]
@@ -101,6 +101,7 @@
 
     top, low = pl.ds(0, half), pl.ds(half, half + POS_ROWS)
     top_a, top_b = pl.ds(0, quarter), pl.ds(quarter, quarter)
+    low_a, low_b = pl.ds(half, quarter), pl.ds(half + quarter, quarter + POS_ROWS)
 
     def kv_copy(k):
         src, dst, dev = (
@@ -109,15 +110,20 @@
             ((0, low), (3, low), x_left),
             ((0, low), (2, low), x_right),
             ((0,), (1,), partner),
-            ((2, top), (6, top), x_right),
-            ((3, low), (6, low), x_left),
+            ((2, top_a), (6, top_a), x_right),
+            ((3, top_b), (6, top_b), x_left),
             ((2,), (4,), partner),
             ((3,), (5,), partner),
-            ((6,), (7,), partner),
+            ((6, top_a), (7, top_a), partner),
             ((0, top_b), (2, top_b), x_right),
             ((0, top_b), (3, top_b), x_left),
+            ((2, low_a), (6, low_a), x_right),
+            ((3, low_b), (6, low_b), x_left),
+            ((6, top_b), (7, top_b), partner),
+            ((6, low_a), (7, low_a), partner),
+            ((6, low_b), (7, low_b), partner),
         )[k]
-        return rc(kv.at[src], kv.at[dst], k if k < 10 else n_ring - 2 + k - 10, dev)
+        return rc(kv.at[src], kv.at[dst], k if k < 10 else n_ring - 7 + k - 10, dev)
 
     y_devs = (y_right, y_left, y_far)
     mine = part_of(cp, piece)
@@ -126,7 +132,10 @@
         return rc(wo_hbm.at[mine, r_cols(at_y((1, -1, 2)[k]))], wr.at[1 + k, mine], 10 + k, y_devs[k])
 
     def we_swap(k):
-        return rc(wo_hbm.at[mine, pl.ds(0, e_cols)], we.at[cp, 1 + k], 13 + k, y_devs[k])
+        if k < 2:
+            return rc(wo_hbm.at[mine, pl.ds(0, e_cols)], we.at[cp, 1 + k], 13 + k, y_devs[k])
+        sub = part_of(k - 2, piece // 2)
+        return rc(we.at[cp, k - 1, sub], we.at[cp, 3, sub], 15 if k == 2 else 16 + 8 * n_tp, y_devs[k - 2])
 
     own, right, left, far = cp, at_x(-1), at_x(1), at_x(2)
     ring = (
@@ -184,14 +193,18 @@
     peers = (x_right, x_left, partner) + y_devs
     for dev in peers:
         pl.semaphore_signal(barrier, inc=1, device_id=dev, device_id_type=MESH)
+    small = [
+        lc(a, b, 6 + N_Q + n_cp + t)
+        for t, (a, b) in enumerate(((pos_hbm, pos_ref), (freq_hbm, freq_ref), (gain_hbm, gain_ref)))
+    ]
+    for cpy in small:
+        cpy.start()
     hid_copy(0).start()
     wk_copy().start()
     wv_copy().start()
-    hid_copy(1).start()
-    hid_copy(2).start()
-    for c in range(N_Q - 2):
-        wq_copy(c).start()
-
+
+    for cpy in small:
+        cpy.wait()
     pos = pos_ref[...]
     pos_row = jnp.concatenate([pos[t : t + 1] for t in range(pos.shape[0])], axis=1)
     pos_q[...] = position_columns(pos_row.astype(jnp.float32))
@@ -212,6 +225,10 @@
         if i == 0:
             wk_copy().wait()
             wv_copy().wait()
+            hid_copy(1).start()
+            hid_copy(2).start()
+            for c in range(N_Q - 2):
+                wq_copy(c).start()
         k = jnp.dot(r[sl, :], wq[N_Q - 2], preferred_element_type=jnp.float32)
         v = jnp.dot(r[sl, :], wq[N_Q - 1], preferred_element_type=jnp.float32).astype(jnp.bfloat16)
         kv[0, sl, kv_cols:] = v
@@ -223,10 +240,10 @@
             pl.semaphore_wait(barrier, len(peers))
             kv_copy(0).start()
             kv_copy(1).start()
+            for t in range(2):
+                we_swap(t).start()
             for t in range(n_tp - 1):
                 wr_swap(t).start()
-            for t in range(n_tp - 1):
-                we_swap(t).start()
         elif i == 1:
             kv_copy(10).start()
             kv_copy(11).start()
@@ -259,20 +276,33 @@
     acc[...] = jnp.zeros_like(acc)
     scale = HEAD**-0.5 * LOG2E
 
-    def attend(i, slot):
-        hi = kv[slot, pl.ds(rows, POS_ROWS // 2), :].astype(jnp.float32)
-        lo = kv[slot, pl.ds(rows + POS_ROWS // 2, POS_ROWS // 2), :].astype(jnp.float32)
-        pos_k = (hi * POS_BASE + lo)[0:1, :]
+    def attend(i, slot, n_blk=1):
         pos_i = pos_q[part_of(i, chunk), :]
-        n_l = rows // HEAD
-        bias = jnp.concatenate(
-            [jnp.where(pos_k[:, t * HEAD : (t + 1) * HEAD] <= pos_i, 0.0, NEG_BIG) for t in range(n_l)], axis=1
-        )
+        n_l = n_blk * rows // HEAD
+        biases = []
+        for b in range(n_blk):
+            hi = kv[slot + b, pl.ds(rows, POS_ROWS // 2), :].astype(jnp.float32)
+            lo = kv[slot + b, pl.ds(rows + POS_ROWS // 2, POS_ROWS // 2), :].astype(jnp.float32)
+            pos_k = (hi * POS_BASE + lo)[0:1, :]
+            for t in range(rows // HEAD):
+                biases.append(jnp.where(pos_k[:, t * HEAD : (t + 1) * HEAD] <= pos_i, 0.0, NEG_BIG))
+        bias = jnp.concatenate(biases, axis=1)
+
+        def block(b, first_col):
+            return kv[slot + b, pl.ds(0, rows), first_col : first_col + HEAD]
+
+        raw = [
+            [
+                lax.dot_general(
+                    q[i, kvh], block(b, kvh * HEAD), (((1,), (1,)), ((), ())), preferred_element_type=jnp.float32
+                )
+                for b in range(n_blk)
+            ]
+            for kvh in range(kv_heads)
+        ]
         for kvh in range(kv_heads):
-            k_blk = kv[slot, pl.ds(0, rows), kvh * HEAD : (kvh + 1) * HEAD]
-            v_blk = kv[slot, pl.ds(0, rows), kv_cols + kvh * HEAD : kv_cols + (kvh + 1) * HEAD]
-            s = lax.dot_general(q[i, kvh], k_blk, (((1,), (1,)), ((), ())), preferred_element_type=jnp.float32)
-            s = (s.reshape(group, chunk, rows) * scale + bias[None]).reshape(group * chunk, rows)
+            s = jnp.concatenate(raw[kvh], axis=1)
+            s = (s.reshape(group, chunk, n_blk * rows) * scale + bias[None]).reshape(group * chunk, n_blk * rows)
             m_old = mx[i, kvh]
             m_new = jnp.maximum(m_old, jnp.max(s, axis=1, keepdims=True))
             alpha = jnp.exp2(m_old - m_new)
@@ -282,16 +312,27 @@
                 part = part + p[:, t * HEAD : (t + 1) * HEAD]
             mx[i, kvh] = m_new
             ls[i, kvh] = ls[i, kvh] * alpha + part
-            acc[i, kvh] = acc[i, kvh] * alpha + jnp.dot(
-                p.astype(jnp.bfloat16), v_blk, preferred_element_type=jnp.float32
-            )
+            p = p.astype(jnp.bfloat16)
+            pv = acc[i, kvh] * alpha
+            for b in range(n_blk):
+                pv = pv + jnp.dot(
+                    p[:, b * rows : (b + 1) * rows], block(b, kv_cols + kvh * HEAD), preferred_element_type=jnp.float32
+                )
+            acc[i, kvh] = pv
 
     n_lead = n_chunk // 2
 
-    def attend_all(chunks, first, n_slot):
+    def attend_each(chunks, slots):
+        n_slot = slots[1] - slots[0]
+
         @pl.loop(0, (chunks[1] - chunks[0]) * n_slot)
         def _(t):
-            attend(chunks[0] + t // n_slot, first + lax.rem(t, n_slot))
+            attend(chunks[0] + t // n_slot, slots[0] + lax.rem(t, n_slot))
+
+    def attend_rest(i, first):
+        @pl.loop(0, (n_cp - first) // 2)
+        def _(t):
+            attend(i, first + 2 * t, 2)
 
     def finish(i):
         for kvh in range(kv_heads):
@@ -303,56 +344,60 @@
         ctx_copy(i, 0).start()
         ctx_copy(i, 1).start()
 
-    attend_all((0, 1), 0, 1)
     kv_copy(0).wait_recv()
+    kv_copy(5).start()
+    attend_each((0, 1), (0, 1))
+    kv_copy(11).wait_recv()
+    kv_copy(6).start()
     kv_copy(10).wait_recv()
-    kv_copy(5).start()
-    attend_all((1, n_lead), 0, 1)
+    kv_copy(1).wait_recv()
+    attend_each((1, n_lead), (0, 1))
+    for k in range(2):
+        we_swap(k).wait_recv()
+        we_swap(2 + k).start()
     kv_copy(4).wait_recv()
-    attend_all((0, n_lead), 1, 1)
+    attend_each((0, n_lead), (1, 2))
+    kv_copy(3).wait_recv()
+    kv_copy(12).start()
+    kv_copy(7).start()
     kv_copy(2).wait_recv()
-    kv_copy(6).start()
-    attend_all((n_lead, n_lead + 1), 0, 2)
+    kv_copy(13).start()
+    kv_copy(8).start()
+    attend_each((n_lead, n_lead + 1), (0, 2))
+    attend_each((0, 1), (2, 4))
+    kv_copy(5).wait_recv()
+    kv_copy(9).start()
+    kv_copy(6).wait_recv()
+    kv_copy(14).start()
+    kv_copy(7).wait_recv()
+    kv_copy(8).wait_recv()
+    attend_each((0, 1), (4, 5))
     for t in range(n_tp - 1):
         wr_swap(t).wait_recv()
-    kv_copy(1).wait_recv()
-    kv_copy(11).wait_recv()
-    kv_copy(3).wait_recv()
-    kv_copy(7).start()
-    kv_copy(8).start()
     start_own(wr_ring)
-    attend_all((0, 1), 2, 2)
-    kv_copy(7).wait_recv()
-    kv_copy(8).wait_recv()
-    attend_all((0, 1), 4, 2)
-    attend_all((1, n_lead), 2, 1)
-    kv_copy(5).wait_recv()
-    kv_copy(6).wait_recv()
-    kv_copy(9).start()
-    attend_all((0, 1), 6, 1)
-    attend_all((1, n_lead), 3, 1)
-    kv_copy(9).wait_recv()
-    attend_all((0, 1), 7, 1)
+    attend_each((0, 1), (5, 6))
+    kv_copy(12).wait_recv()
+    kv_copy(15).start()
+    kv_copy(13).wait_recv()
+    kv_copy(16).start()
+    attend_each((0, 1), (6, 7))
+    for k in (9, 14, 15, 16):
+        kv_copy(k).wait_recv()
+    attend_each((0, 1), (7, 8))
     finish(0)
 
     @pl.loop(1, n_lead)
     def _(i):
-        @pl.loop(4, n_cp)
-        def _(slot):
-            attend(i, slot)
-
+        attend_rest(i, 2)
         finish(i)
 
     we_k = lambda k: functools.partial(we_ring, k)
-    for k in range(n_tp - 1):
+    for k in range(2, 4):
         we_swap(k).wait_recv()
     start_own(we_k(1))
 
     def late_chunk(i, first):
-        @pl.loop(first, n_cp)
-        def _(slot):
-            attend(i, slot)
-
+        attend_rest(i, first)
         finish(i)
         forward(ctx_copy, i - n_lead)
 
@@ -364,14 +409,11 @@
     pass_on(we_k(1))
     forward(ctx_copy, n_lead)
     pass_far(wr_ring)
-    pass_on(we_k(2))
-    forward(ctx_copy, n_lead + 1)
     for m in (2, 5, 6, 7):
         wr_ring(m).wait_recv()
     wr_copy().wait()
 
-    @pl.loop(0, n_chunk)
-    def _(i):
+    def project_own(i):
         ctx_copy(i, 2).wait_recv()
         ctx_copy(i, 3).wait_recv()
         sl = part_of(i, chunk)
@@ -381,6 +423,13 @@
         out[sl, r_cols(tp)] = (out[sl, r_cols(tp)].astype(jnp.float32) + proj).astype(jnp.bfloat16)
         res_copy(i, 0).start()
         res_copy(i, 1).start()
+
+    project_loop = lambda lo, hi: pl.loop(lo, hi)(project_own)
+    project_loop(0, n_chunk - 3)
+    forward(ctx_copy, n_lead + 1)
+    project_loop(n_chunk - 3, n_chunk - 2)
+    pass_on(we_k(2))
+    project_loop(n_chunk - 2, n_chunk)
 
     e_tile = 512
     n_e = e_cols // e_tile
@@ -432,10 +481,11 @@
         res_copy(i, 2).wait_recv()
         res_copy(i, 3).wait_recv()
 
-    for k in range(12):
+    for k in range(17):
         kv_copy(k).wait_send()
     for k in range(n_tp - 1):
         wr_swap(k).wait_send()
+    for k in range(4):
         we_swap(k).wait_send()
     for m in range(8):
         wr_ring(m).wait_send()
@@ -460,12 +510,12 @@
     cols = (width - e_cols) // n_tp
     k_rows = w_out.shape[0]
     bf16, f32 = jnp.bfloat16, jnp.float32
-    n_sem = 18 + 8 * n_tp + 8 * n_chunk
+    n_sem = 24 + 8 * n_tp + 8 * n_chunk
     cache = (rows, kv_heads, HEAD)
     return pl.pallas_call(
         functools.partial(block_kernel, n_tp, n_cp // 2),
         out_shape=[pltpu.VMEM(s, bf16) for s in ((rows, width), cache, cache)],
-        in_specs=[vmem_spec()] * 3 + [any_spec()] * 5,
+        in_specs=[any_spec()] * 8,
         out_specs=[vmem_spec()] * 3,
         scratch_shapes=[
             pltpu.VMEM((n_cp, rows + POS_ROWS, 2 * kv_cols), bf16),
@@ -482,9 +532,12 @@
             pltpu.VMEM((n_chunk, kv_heads, grp, HEAD), f32),
             pltpu.VMEM((rows, e_cols), f32),
             pltpu.VMEM((rows, HEAD), f32),
+            pltpu.VMEM(pos.shape, pos.dtype),
+            pltpu.VMEM(freq.shape, f32),
+            pltpu.VMEM(gain.shape, f32),
             pltpu.SemaphoreType.DMA((n_sem,)),
             pltpu.SemaphoreType.DMA((n_sem,)),
-            pltpu.SemaphoreType.DMA((6 + N_Q + n_cp,)),
+            pltpu.SemaphoreType.DMA((9 + N_Q + n_cp,)),
         ],
         compiler_params=pltpu.CompilerParams(collective_id=0, has_side_effects=True, vmem_limit_bytes=VMEM_LIMIT - 5 * 2**20),
         name="attention_block",

time: 96.1 us -> 94.3 us (0.981)
  Pallas kernels: 95.2 us -> 93.4 us
    pallas_call x1, Pallas kernels: 92.9 us -> 91.2 us  [attention_block(): pl.pallas_call(functools.partial(block_kernel, n_tp, n_cp // 2), out_shap...]
where the time goes in v5:
time: 94.3 us
  Pallas kernels  93.4 us (99%)
    pallas_call x1, Pallas kernels, attention_block(): pl.pallas_call(functools.partial(block_kernel, n_tp, n_cp // 2), out_shap...  91.2 us
    pallas_call x1, Pallas kernels, copy_out(): pl.pallas_call(copy_kernel, in_specs=[vmem_spec()] * 3, out_specs=[any_sp...  2.24 us

profile of v5, /device:TPU:97, one launch (start us, length us, event | category | flops | bytes accessed | tf_op | source)
XLA Modules:
  0.0 94.3 jit_solution(8916287573969537770)
XLA Ops:
  0.6 91.2 %attention_block.1 = (bf16[512,4096]{1,0:T(8,128)(2,1)S(1)}, bf16[512,2,128]{2,1,0:T(2,128)(2,1)S(1)}, bf16[512,2,128]{2,1,0:T(2,128)(2,1)S(1)}) custom-call(s32[4,128]{1,0:T(4,128)} %bitcast.3, f32[1,128]{1,0:T(1,128)} %constant.2.clone.freq_hbm, f32[1,4096]{1,0:T(1,128)} %bitcast.2, bf16[512,4096]{1,0:T(8,128)(2,1)} %hid_hbm.1, bf16[4096,256]{1,0:T(8,128)(2,1)} %wk_hbm.1, ...), custom_call_target="tpu_custom_call" | custom-call | tf_op jit(solution)/shard_map/attention_block/pallas_call | solution.py:515
  91.8 2.2 %copy_out.1 = (bf16[512,4096]{1,0:T(8,128)(2,1)}, bf16[512,2,128]{2,1,0:T(2,128)(2,1)}, bf16[512,2,128]{2,1,0:T(2,128)(2,1)}) custom-call(bf16[512,4096]{1,0:T(8,128)(2,1)S(1)} %get-tuple-element.6.src, bf16[512,2,128]{2,1,0:T(2,128)(2,1)S(1)} %get-tuple-element.7.k_src, bf16[512,2,128]{2,1,0:T(2,128)(2,1)S(1)} %get-tuple-element.8.v_src), custom_call_target="tpu_custom_call" | custom-call | tf_op jit(solution)/shard_map/copy_out/pallas_call | solution.py:562

commit v6 on v5

--- a/solution.py
+++ b/solution.py
@@ -58,7 +58,8 @@
     group = heads // kv_heads
     n_chunk, chunk = mx.shape[0], mx.shape[2] // group
     n_cp = 2 * n_x
-    n_ring = 24 + 8 * n_tp
+    n_hop = 9
+    n_ring = 26 + n_hop * n_tp
     half = rows // 2
     cols = wr.shape[2]
     e_cols = we.shape[3]
@@ -76,9 +77,14 @@
     x_right, x_left, partner = {"cp": at_x(1)}, {"cp": at_x(-1)}, {"cp": at_x(0, 1)}
     y_right, y_left, y_far = {"tp": at_y(1)}, {"tp": at_y(-1)}, {"tp": at_y(2)}
 
-    def rc(src, dst, idx, dev):
+    def rc(src, dst, idx, dev, send=None):
         return pltpu.make_async_remote_copy(
-            src_ref=src, dst_ref=dst, send_sem=ssem.at[idx], recv_sem=rsem.at[idx], device_id=dev, device_id_type=MESH
+            src_ref=src,
+            dst_ref=dst,
+            send_sem=ssem.at[idx if send is None else send],
+            recv_sem=rsem.at[idx],
+            device_id=dev,
+            device_id_type=MESH,
         )
 
     def lc(src, dst, idx):
@@ -101,12 +107,13 @@
 
     top, low = pl.ds(0, half), pl.ds(half, half + POS_ROWS)
     top_a, top_b = pl.ds(0, quarter), pl.ds(quarter, quarter)
+    k_cols, v_cols = pl.ds(0, kv_cols), pl.ds(kv_cols, kv_cols)
     low_a, low_b = pl.ds(half, quarter), pl.ds(half + quarter, quarter + POS_ROWS)
 
     def kv_copy(k):
         src, dst, dev = (
-            ((0, top_a), (2, top_a), x_right),
-            ((0, top_a), (3, top_a), x_left),
+            ((0, top_a, v_cols), (2, top_a, v_cols), x_right),
+            ((0, top_a, v_cols), (3, top_a, v_cols), x_left),
             ((0, low), (3, low), x_left),
             ((0, low), (2, low), x_right),
             ((0,), (1,), partner),
@@ -122,8 +129,10 @@
             ((6, top_b), (7, top_b), partner),
             ((6, low_a), (7, low_a), partner),
             ((6, low_b), (7, low_b), partner),
+            ((0, top_a, k_cols), (2, top_a, k_cols), x_right),
+            ((0, top_a, k_cols), (3, top_a, k_cols), x_left),
         )[k]
-        return rc(kv.at[src], kv.at[dst], k if k < 10 else n_ring - 7 + k - 10, dev)
+        return rc(kv.at[src], kv.at[dst], k if k < 10 else n_ring - 9 + k - 10, dev)
 
     y_devs = (y_right, y_left, y_far)
     mine = part_of(cp, piece)
@@ -135,12 +144,12 @@
         if k < 2:
             return rc(wo_hbm.at[mine, pl.ds(0, e_cols)], we.at[cp, 1 + k], 13 + k, y_devs[k])
         sub = part_of(k - 2, piece // 2)
-        return rc(we.at[cp, k - 1, sub], we.at[cp, 3, sub], 15 if k == 2 else 16 + 8 * n_tp, y_devs[k - 2])
+        return rc(we.at[cp, k - 1, sub], we.at[cp, 3, sub], 15 if k == 2 else 16 + n_hop * n_tp, y_devs[k - 2])
 
     own, right, left, far = cp, at_x(-1), at_x(1), at_x(2)
     ring = (
         (own, x_right, None), (own, x_left, None), (own, partner, None), (right, x_right, 0), (left, x_left, 1),
-        (right, partner, None), (left, partner, None), (far, partner, None),
+        (right, partner, None), (left, partner, None), (far, partner, 0), (far, partner, 1),
     )
 
     def wr_ring(m):
@@ -151,7 +160,7 @@
     def we_ring(k, m):
         src, dev, sub = ring[m]
         ref = we.at[src, k] if sub is None else we.at[src, k, part_of(sub, piece // 2)]
-        return rc(ref, ref, 16 + 8 * k + m, dev)
+        return rc(ref, ref, 16 + n_hop * k + m, dev)
 
     def start_own(copy):
         for m in range(3):
@@ -167,8 +176,9 @@
 
     def pass_far(copy):
         copy(3).wait_recv()
+        copy(7).start()
         copy(4).wait_recv()
-        copy(7).start()
+        copy(8).start()
 
     ctx_base = n_ring
     out_base = ctx_base + 4 * n_chunk
@@ -176,18 +186,23 @@
     def ctx_copy(i, k):
         src, dst, sub, dev = ((0, 1, None, y_right), (0, 2, None, y_left), (1, 3, 0, y_right), (2, 3, 1, y_left))[k]
         sl = part_of(i, chunk, sub)
-        return rc(ct.at[src, sl], ct.at[dst, sl], ctx_base + 4 * i + k, dev)
+        return rc(ct.at[src, sl], ct.at[dst, sl], ctx_base + 4 * i + k, dev, 4 * i + k)
 
     def res_copy(i, k):
         t, sub, dev = ((tp, None, y_right), (tp, None, y_left), (at_y(-1), 0, y_right), (at_y(1), 1, y_left))[k]
         ref = out.at[part_of(i, chunk, sub), r_cols(t)]
-        return rc(ref, ref, out_base + 4 * i + k, dev)
+        return rc(ref, ref, out_base + 4 * i + k, dev, 4 * i + k)
 
     def forward(copy, i):
         copy(i, 0).wait_recv()
         copy(i, 2).start()
         copy(i, 1).wait_recv()
         copy(i, 3).start()
+
+    def forward_res(i):
+        ctx_copy(i, 2).wait_send()
+        ctx_copy(i, 3).wait_send()
+        forward(res_copy, i)
 
     barrier = pltpu.get_barrier_semaphore()
     peers = (x_right, x_left, partner) + y_devs
@@ -195,16 +210,59 @@
         pl.semaphore_signal(barrier, inc=1, device_id=dev, device_id_type=MESH)
     small = [
         lc(a, b, 6 + N_Q + n_cp + t)
-        for t, (a, b) in enumerate(((pos_hbm, pos_ref), (freq_hbm, freq_ref), (gain_hbm, gain_ref)))
+        for t, (a, b) in enumerate(((gain_hbm, gain_ref), (pos_hbm, pos_ref), (freq_hbm, freq_ref)))
     ]
-    for cpy in small:
-        cpy.start()
+    small[0].start()
     hid_copy(0).start()
+    wv_copy().start()
     wk_copy().start()
-    wv_copy().start()
-
-    for cpy in small:
-        cpy.wait()
+    small[1].start()
+    small[2].start()
+    hid_copy(1).start()
+    hid_copy(2).start()
+    for c in range(N_Q - 2):
+        wq_copy(c).start()
+
+    def normalise(sl):
+        hid = out[sl, :].astype(jnp.float32)
+        scaled = hid * lax.rsqrt(jnp.mean(hid * hid, axis=-1, keepdims=True) + EPS)
+        r[sl, :] = (scaled * gain_ref[...]).astype(jnp.bfloat16)
+
+    def product(sl, w):
+        return jnp.dot(r[sl, :], wq[w], preferred_element_type=jnp.float32)
+
+    def put_v(sl, v):
+        v = v.astype(jnp.bfloat16)
+        kv[0, sl, kv_cols:] = v
+        vc[sl] = jnp.stack([v[:, h * HEAD : (h + 1) * HEAD] for h in range(kv_heads)], axis=1)
+
+    def put_k(sl, k):
+        rots = []
+        for h in range(kv_heads):
+            rots.append(rope(k[:, h * HEAD : (h + 1) * HEAD], cos[sl, :], sin[sl, :]))
+            kv[0, sl, h * HEAD : (h + 1) * HEAD] = rots[h]
+        kc[sl] = jnp.stack(rots, axis=1)
+
+    def project_kv(sl):
+        k, v = product(sl, N_Q - 2), product(sl, N_Q - 1)
+        put_v(sl, v)
+        put_k(sl, k)
+
+    small[0].wait()
+    hid_copy(0).wait()
+    normalise(parts[0])
+    wv_copy().wait()
+    put_v(parts[0], product(parts[0], N_Q - 1))
+    pl.semaphore_wait(barrier, len(peers))
+    kv_copy(0).start()
+    kv_copy(1).start()
+    for t in range(2):
+        we_swap(t).start()
+    for t in range(n_tp - 1):
+        wr_swap(t).start()
+
+    small[1].wait()
+    small[2].wait()
     pos = pos_ref[...]
     pos_row = jnp.concatenate([pos[t : t + 1] for t in range(pos.shape[0])], axis=1)
     pos_q[...] = position_columns(pos_row.astype(jnp.float32))
@@ -217,42 +275,21 @@
     lo = jnp.broadcast_to(lax.rem(pos_row, POS_BASE).astype(jnp.float32), (POS_ROWS // 2, rows))
     kv[0, rows:, :] = jnp.concatenate([hi, lo], axis=0).astype(jnp.bfloat16)
 
-    for i, sl in enumerate(parts):
-        hid_copy(i).wait()
-        hid = out[sl, :].astype(jnp.float32)
-        scaled = hid * lax.rsqrt(jnp.mean(hid * hid, axis=-1, keepdims=True) + EPS)
-        r[sl, :] = (scaled * gain_ref[...]).astype(jnp.bfloat16)
-        if i == 0:
-            wk_copy().wait()
-            wv_copy().wait()
-            hid_copy(1).start()
-            hid_copy(2).start()
-            for c in range(N_Q - 2):
-                wq_copy(c).start()
-        k = jnp.dot(r[sl, :], wq[N_Q - 2], preferred_element_type=jnp.float32)
-        v = jnp.dot(r[sl, :], wq[N_Q - 1], preferred_element_type=jnp.float32).astype(jnp.bfloat16)
-        kv[0, sl, kv_cols:] = v
-        rots = []
-        for h in range(kv_heads):
-            rots.append(rope(k[:, h * HEAD : (h + 1) * HEAD], cos[sl, :], sin[sl, :]))
-            kv[0, sl, h * HEAD : (h + 1) * HEAD] = rots[h]
-        if i == 0:
-            pl.semaphore_wait(barrier, len(peers))
-            kv_copy(0).start()
-            kv_copy(1).start()
-            for t in range(2):
-                we_swap(t).start()
-            for t in range(n_tp - 1):
-                wr_swap(t).start()
-        elif i == 1:
-            kv_copy(10).start()
-            kv_copy(11).start()
-        else:
-            kv_copy(2).start()
-            kv_copy(3).start()
-            kv_copy(4).start()
-        kc[sl] = jnp.stack(rots, axis=1)
-        vc[sl] = jnp.stack([v[:, h * HEAD : (h + 1) * HEAD] for h in range(kv_heads)], axis=1)
+    wk_copy().wait()
+    put_k(parts[0], product(parts[0], N_Q - 2))
+    kv_copy(17).start()
+    kv_copy(18).start()
+    hid_copy(1).wait()
+    normalise(parts[1])
+    project_kv(parts[1])
+    kv_copy(10).start()
+    kv_copy(11).start()
+    hid_copy(2).wait()
+    normalise(parts[2])
+    project_kv(parts[2])
+    kv_copy(2).start()
+    kv_copy(3).start()
+    kv_copy(4).start()
     for c in range(N_Q - 2, N_Q):
         wq_copy(c).start()
     wr_copy().start()
@@ -329,8 +366,8 @@
         def _(t):
             attend(chunks[0] + t // n_slot, slots[0] + lax.rem(t, n_slot))
 
-    def attend_rest(i, first):
-        @pl.loop(0, (n_cp - first) // 2)
+    def attend_some(i, first, last):
+        @pl.loop(0, (last - first) // 2)
         def _(t):
             attend(i, first + 2 * t, 2)
 
@@ -345,25 +382,27 @@
         ctx_copy(i, 1).start()
 
     kv_copy(0).wait_recv()
+    kv_copy(17).wait_recv()
     kv_copy(5).start()
     attend_each((0, 1), (0, 1))
     kv_copy(11).wait_recv()
     kv_copy(6).start()
     kv_copy(10).wait_recv()
     kv_copy(1).wait_recv()
+    kv_copy(18).wait_recv()
     attend_each((1, n_lead), (0, 1))
     for k in range(2):
         we_swap(k).wait_recv()
         we_swap(2 + k).start()
     kv_copy(4).wait_recv()
-    attend_each((0, n_lead), (1, 2))
+    attend_each((0, 1), (1, 2))
     kv_copy(3).wait_recv()
     kv_copy(12).start()
     kv_copy(7).start()
     kv_copy(2).wait_recv()
     kv_copy(13).start()
     kv_copy(8).start()
-    attend_each((n_lead, n_lead + 1), (0, 2))
+    attend_each((1, n_lead), (1, 2))
     attend_each((0, 1), (2, 4))
     kv_copy(5).wait_recv()
     kv_copy(9).start()
@@ -384,11 +423,16 @@
     for k in (9, 14, 15, 16):
         kv_copy(k).wait_recv()
     attend_each((0, 1), (7, 8))
+    for k in range(19):
+        kv_copy(k).wait_send()
+    for k in range(n_tp - 1):
+        wr_swap(k).wait_send()
+        we_swap(k).wait_send()
     finish(0)
 
     @pl.loop(1, n_lead)
     def _(i):
-        attend_rest(i, 2)
+        attend_some(i, 2, n_cp)
         finish(i)
 
     we_k = lambda k: functools.partial(we_ring, k)
@@ -396,20 +440,21 @@
         we_swap(k).wait_recv()
     start_own(we_k(1))
 
-    def late_chunk(i, first):
-        attend_rest(i, first)
+    def late_chunk(i):
+        attend_some(i, 0, n_cp // 2)
+        forward(ctx_copy, i - n_lead)
+        attend_some(i, n_cp // 2, n_cp)
         finish(i)
-        forward(ctx_copy, i - n_lead)
-
-    late_chunk(n_lead, 2)
+
+    late_chunk(n_lead)
     pass_on(wr_ring)
     for k in range(2, n_tp):
         start_own(we_k(k))
-    late_chunk(n_lead + 1, 0)
+    late_chunk(n_lead + 1)
     pass_on(we_k(1))
     forward(ctx_copy, n_lead)
     pass_far(wr_ring)
-    for m in (2, 5, 6, 7):
+    for m in (2, 5, 6, 7, 8):
         wr_ring(m).wait_recv()
     wr_copy().wait()
 
@@ -421,8 +466,9 @@
         for t in range(1, n_tp):
             proj = proj + jnp.dot(ct[t, sl, :], wr[t], preferred_element_type=jnp.float32)
         out[sl, r_cols(tp)] = (out[sl, r_cols(tp)].astype(jnp.float32) + proj).astype(jnp.bfloat16)
-        res_copy(i, 0).start()
-        res_copy(i, 1).start()
+        for k in range(2):
+            ctx_copy(i, k).wait_send()
+            res_copy(i, k).start()
 
     project_loop = lambda lo, hi: pl.loop(lo, hi)(project_own)
     project_loop(0, n_chunk - 3)
@@ -453,27 +499,28 @@
         we_copy(j).wait()
     pass_on(we_k(3))
     project(own, first=True)
-    forward(res_copy, 0)
+    forward_res(0)
     for k in range(1, n_tp):
         we_k(k)(2).wait_recv()
     project(at_x(0, 1))
     project(right)
-    forward(res_copy, 1)
+    forward_res(1)
     pass_far(we_k(1))
     project(left)
-    forward(res_copy, 2)
+    forward_res(2)
     pass_far(we_k(2))
     for k in range(1, n_tp):
         we_k(k)(5).wait_recv()
     project(at_x(-1, 1))
     for k in range(1, n_tp):
         we_k(k)(6).wait_recv()
-    forward(res_copy, 3)
+    forward_res(3)
+    project(at_x(1, 1))
     pass_far(we_k(3))
-    project(at_x(1, 1))
     project(far)
     for k in range(1, n_tp):
         we_k(k)(7).wait_recv()
+        we_k(k)(8).wait_recv()
     project(at_x(2, 1), last=True)
 
     @pl.loop(0, n_chunk)
@@ -481,13 +528,8 @@
         res_copy(i, 2).wait_recv()
         res_copy(i, 3).wait_recv()
 
-    for k in range(17):
-        kv_copy(k).wait_send()
-    for k in range(n_tp - 1):
-        wr_swap(k).wait_send()
-    for k in range(4):
-        we_swap(k).wait_send()
-    for m in range(8):
+    we_swap(3).wait_send()
+    for m in range(n_hop):
         wr_ring(m).wait_send()
         for k in range(1, n_tp):
             we_ring(k, m).wait_send()
@@ -495,7 +537,6 @@
     @pl.loop(0, n_chunk)
     def _(i):
         for k in range(4):
-            ctx_copy(i, k).wait_send()
             res_copy(i, k).wait_send()
 
 
@@ -510,7 +551,7 @@
     cols = (width - e_cols) // n_tp
     k_rows = w_out.shape[0]
     bf16, f32 = jnp.bfloat16, jnp.float32
-    n_sem = 24 + 8 * n_tp + 8 * n_chunk
+    n_sem = 26 + 9 * n_tp + 8 * n_chunk
     cache = (rows, kv_heads, HEAD)
     return pl.pallas_call(
         functools.partial(block_kernel, n_tp, n_cp // 2),
@@ -535,7 +576,7 @@
             pltpu.VMEM(pos.shape, pos.dtype),
             pltpu.VMEM(freq.shape, f32),
             pltpu.VMEM(gain.shape, f32),
-            pltpu.SemaphoreType.DMA((n_sem,)),
+            pltpu.SemaphoreType.DMA((n_sem - 8 * n_chunk,)),
             pltpu.SemaphoreType.DMA((n_sem,)),
             pltpu.SemaphoreType.DMA((9 + N_Q + n_cp,)),
         ],

time: 94.3 us -> 93.7 us (level)
  no operation moved by 1% of the time
where the time goes in v6:
time: 93.7 us; the launch traced here: 93.5 us
  Pallas kernels  92.7 us (99%)
    pallas_call x1, Pallas kernels, attention_block(): pl.pallas_call(functools.partial(block_kernel, n_tp, n_cp // 2), out_shap...  90.4 us
    pallas_call x1, Pallas kernels, copy_out(): pl.pallas_call(copy_kernel, in_specs=[vmem_spec()] * 3, out_specs=[any_sp...  2.24 us

profile of v6, /device:TPU:97, one launch (start us, length us, event | category | flops | bytes accessed | tf_op | source)
XLA Modules:
  0.0 93.5 jit_solution(16603834883414138810)
XLA Ops:
  0.6 90.4 %attention_block.1 = (bf16[512,4096]{1,0:T(8,128)(2,1)S(1)}, bf16[512,2,128]{2,1,0:T(2,128)(2,1)S(1)}, bf16[512,2,128]{2,1,0:T(2,128)(2,1)S(1)}) custom-call(s32[4,128]{1,0:T(4,128)} %bitcast.3, f32[1,128]{1,0:T(1,128)} %constant.2.clone.freq_hbm, f32[1,4096]{1,0:T(1,128)} %bitcast.2, bf16[512,4096]{1,0:T(8,128)(2,1)} %hid_hbm.1, bf16[4096,256]{1,0:T(8,128)(2,1)} %wk_hbm.1, ...), custom_call_target="tpu_custom_call" | custom-call | tf_op jit(solution)/shard_map/attention_block/pallas_call | solution.py:556
  91.1 2.2 %copy_out.1 = (bf16[512,4096]{1,0:T(8,128)(2,1)}, bf16[512,2,128]{2,1,0:T(2,128)(2,1)}, bf16[512,2,128]{2,1,0:T(2,128)(2,1)}) custom-call(bf16[512,4096]{1,0:T(8,128)(2,1)S(1)} %get-tuple-element.6.src, bf16[512,2,128]{2,1,0:T(2,128)(2,1)S(1)} %get-tuple-element.7.k_src, bf16[512,2,128]{2,1,0:T(2,128)(2,1)S(1)} %get-tuple-element.8.v_src), custom_call_target="tpu_custom_call" | custom-call | tf_op jit(solution)/shard_map/copy_out/pallas_call | solution.py:603

commit v7 on v6

--- a/solution.py
+++ b/solution.py
@@ -256,10 +256,10 @@
     pl.semaphore_wait(barrier, len(peers))
     kv_copy(0).start()
     kv_copy(1).start()
+    for t in range(n_tp - 1):
+        wr_swap(t).start()
     for t in range(2):
         we_swap(t).start()
-    for t in range(n_tp - 1):
-        wr_swap(t).start()
 
     small[1].wait()
     small[2].wait()
@@ -391,9 +391,6 @@
     kv_copy(1).wait_recv()
     kv_copy(18).wait_recv()
     attend_each((1, n_lead), (0, 1))
-    for k in range(2):
-        we_swap(k).wait_recv()
-        we_swap(2 + k).start()
     kv_copy(4).wait_recv()
     attend_each((0, 1), (1, 2))
     kv_copy(3).wait_recv()
@@ -410,6 +407,9 @@
     kv_copy(14).start()
     kv_copy(7).wait_recv()
     kv_copy(8).wait_recv()
+    for k in range(2):
+        we_swap(k).wait_recv()
+        we_swap(2 + k).start()
     attend_each((0, 1), (4, 5))
     for t in range(n_tp - 1):
         wr_swap(t).wait_recv()

time: 93.7 us -> 93.5 us (level)
  no operation moved by 1% of the time
where the time goes in v7:
time: 93.5 us; the launch traced here: 93.4 us
  Pallas kernels  92.6 us (99%)
    pallas_call x1, Pallas kernels, attention_block(): pl.pallas_call(functools.partial(block_kernel, n_tp, n_cp // 2), out_shap...  90.3 us
    pallas_call x1, Pallas kernels, copy_out(): pl.pallas_call(copy_kernel, in_specs=[vmem_spec()] * 3, out_specs=[any_sp...  2.24 us

profile of v7, /device:TPU:97, one launch (start us, length us, event | category | flops | bytes accessed | tf_op | source)
XLA Modules:
  0.0 93.4 jit_solution(4647231071356667736)
XLA Ops:
  0.6 90.3 %attention_block.1 = (bf16[512,4096]{1,0:T(8,128)(2,1)S(1)}, bf16[512,2,128]{2,1,0:T(2,128)(2,1)S(1)}, bf16[512,2,128]{2,1,0:T(2,128)(2,1)S(1)}) custom-call(s32[4,128]{1,0:T(4,128)} %bitcast.3, f32[1,128]{1,0:T(1,128)} %constant.2.clone.freq_hbm, f32[1,4096]{1,0:T(1,128)} %bitcast.2, bf16[512,4096]{1,0:T(8,128)(2,1)} %hid_hbm.1, bf16[4096,256]{1,0:T(8,128)(2,1)} %wk_hbm.1, ...), custom_call_target="tpu_custom_call" | custom-call | tf_op jit(solution)/shard_map/attention_block/pallas_call | solution.py:556
  91.0 2.2 %copy_out.1 = (bf16[512,4096]{1,0:T(8,128)(2,1)}, bf16[512,2,128]{2,1,0:T(2,128)(2,1)}, bf16[512,2,128]{2,1,0:T(2,128)(2,1)}) custom-call(bf16[512,4096]{1,0:T(8,128)(2,1)S(1)} %get-tuple-element.6.src, bf16[512,2,128]{2,1,0:T(2,128)(2,1)S(1)} %get-tuple-element.7.k_src, bf16[512,2,128]{2,1,0:T(2,128)(2,1)S(1)} %get-tuple-element.8.v_src), custom_call_target="tpu_custom_call" | custom-call | tf_op jit(solution)/shard_map/copy_out/pallas_call | solution.py:603
